TPU v7x, 16 devices: a whole 2x2x2 slice. The times are simulated.
16 devices in a mesh: nodes: 16 (over z, y, x, core).
Axes of the slice: x: 2, y: 2, z: 2, core: 2. Of those that a mesh axis runs over, the one named last changes fastest.
Arguments:
- adjacency: bfloat16 [16384, 16384], P('nodes')
- features: bfloat16 [16384, 100], P('nodes')
- w_hidden: float32 [100, 128], replicated
- w_output: float32 [128, 47], replicated
- labels: int32 [16384], P('nodes')
- train_mask: int32 [16384], P('nodes')
- block_mask: int32 [16, 16], replicated
Outputs:
- output 1: float32 [], replicated
- output 2: float32 [100, 128], replicated
- output 3: float32 [128, 47], replicated
All inputs are finite; a program needn't handle non-finite values.
Results may differ from a plain program's by a relative error of at most 0.001.
Values are sent between devices in bfloat16 or wider.
A program may use at most 1 GiB of HBM per device.

v0:
```python
import jax
import jax.numpy as jnp
from jax import lax
from jax.sharding import PartitionSpec as P

AXIS_NAME = 'nodes'
ROW_CONTRACT = (((0,), (0,)), ((), ()))
LAST_CONTRACT = (((1,), (1,)), ((), ()))


def gather_masked(local_vals, mask_row):
    gathered = lax.all_gather(local_vals, AXIS_NAME, axis=0, tiled=False)
    gathered = gathered * mask_row.astype(local_vals.dtype)[:, None, None]
    return gathered.reshape(-1, local_vals.shape[-1])


def transpose_product_scatter(adj_rows, local_grad, mask_row):
    width = local_grad.shape[-1]
    contrib = lax.dot_general(adj_rows, local_grad, ROW_CONTRACT, preferred_element_type=jnp.float32)
    contrib = contrib.reshape(mask_row.shape[0], -1, width) * mask_row.astype(jnp.float32)[:, None, None]
    return lax.psum_scatter(contrib.reshape(-1, width), AXIS_NAME, scatter_dimension=0, tiled=True)


def device_step(adj_rows, feat_rows, w_hidden, w_output, labels, train_mask, block_mask):
    dev_index = lax.axis_index(AXIS_NAME)
    mask_row = lax.dynamic_index_in_dim(block_mask, dev_index, axis=0, keepdims=False)
    w_hidden_bf = w_hidden.astype(jnp.bfloat16)
    w_output_bf = w_output.astype(jnp.bfloat16)
    proj_one = jnp.dot(feat_rows, w_hidden_bf, preferred_element_type=jnp.float32).astype(jnp.bfloat16)
    agg_one = jnp.dot(adj_rows, gather_masked(proj_one, mask_row), preferred_element_type=jnp.float32)
    hidden = jnp.maximum(agg_one, 0.0).astype(jnp.bfloat16)
    proj_two = jnp.dot(hidden, w_output_bf, preferred_element_type=jnp.float32).astype(jnp.bfloat16)
    logits = jnp.dot(adj_rows, gather_masked(proj_two, mask_row), preferred_element_type=jnp.float32)
    label_weight = train_mask.astype(jnp.float32)
    log_norm = jax.nn.logsumexp(logits, axis=-1)
    one_hot = (labels[:, None] == jnp.arange(logits.shape[-1])[None, :]).astype(jnp.float32)
    picked = jnp.sum(logits * one_hot, axis=-1)
    totals = lax.psum(jnp.stack([jnp.sum(label_weight), jnp.sum(label_weight * (log_norm - picked))]), AXIS_NAME)
    label_count = totals[0]
    mean_loss = totals[1] / label_count
    probabilities = jnp.exp(logits - log_norm[:, None])
    grad_logits = ((probabilities - one_hot) * (label_weight / label_count)[:, None]).astype(jnp.bfloat16)
    grad_proj_two = transpose_product_scatter(adj_rows, grad_logits, mask_row).astype(jnp.bfloat16)
    grad_w_output = lax.psum(lax.dot_general(hidden, grad_proj_two, ROW_CONTRACT, preferred_element_type=jnp.float32), AXIS_NAME)
    grad_hidden = lax.dot_general(grad_proj_two, w_output_bf, LAST_CONTRACT, preferred_element_type=jnp.float32)
    grad_agg = jnp.where(agg_one > 0, grad_hidden, 0.0).astype(jnp.bfloat16)
    grad_proj_one = transpose_product_scatter(adj_rows, grad_agg, mask_row).astype(jnp.bfloat16)
    grad_w_hidden = lax.psum(lax.dot_general(feat_rows, grad_proj_one, ROW_CONTRACT, preferred_element_type=jnp.float32), AXIS_NAME)
    return mean_loss, grad_w_hidden, grad_w_output


def solution(mesh):
    row_spec = P(AXIS_NAME, None)
    vec_spec = P(AXIS_NAME)
    return jax.shard_map(device_step, mesh=mesh, in_specs=(row_spec, row_spec, P(), P(), vec_spec, vec_spec, P()), out_specs=(P(), P(), P()), check_vma=False)
```

profile of v0, /device:TPU:0, one launch (start us, length us, event | category | flops | bytes accessed | tf_op | source)
XLA Modules:
  0.0 408.5 jit_solution(6883730668524531056)
XLA Ops:
  7.2 0.9 copy-done
  8.1 1.8 convolution_convert_fusion
  9.9 0.7 convert_bitcast_fusion
  10.6 37.5 %all-gather.5.cloned.1.call-done = bf16[16384,128]{1,0:T(8,128)(2,1)} async-done(((bf16[1024,128]{1,0:T(8,128)(2,1)}), bf16[16384,128]{1,0:T(8,128)(2,1)}) %all-gather.5.cloned.1.call-update) | async-done | bytes 4194320 | tf_op jit(solution)/shard_map/all_gather | solution.py:12
  48.1 2.5 broadcast_multiply_fusion
  50.7 16.1 %fusion.33 = f32[128,1024]{1,0:T(8,128)S(1)} fusion(bf16[16384,128]{1,0:T(8,128)(2,1)S(1)} %bitcast.65, bf16[1024,16384]{1,0:T(8,128)(2,1)} %param.7), kind=kOutput, calls=%fused_computation.53 | convolution fusion | flops 4294967296 | bytes 38273024 | tf_op jit(solution)/shard_map/dot_general | solution.py:30
  66.8 0.8 convolution_convert_fusion.1
  67.7 27.3 %all-gather.7.cloned.1.call-done = bf16[16384,47]{0,1:T(8,128)(2,1)} async-done(((bf16[1024,47]{0,1:T(8,128)(2,1)}), bf16[16384,47]{0,1:T(8,128)(2,1)}) %all-gather.7.cloned.1.call-update) | async-done | bytes 1540112 | tf_op jit(solution)/shard_map/all_gather | solution.py:12
  95.0 2.3 copy.10
  97.7 0.9 copy.11
  98.7 15.2 %fusion.32 = (f32[1024]{0:T(1024)S(1)}, f32[47,1024]{1,0:T(8,128)S(1)}) fusion(bf16[16384,47]{0,1:T(8,128)(2,1)S(1)} %bitcast.66, bf16[1024,16384]{1,0:T(8,128)(2,1)} %param.7), kind=kOutput, calls=%fused_computation.52 | convolution fusion | flops 1577105408 | bytes 35291136 | tf_op jit(solution)/shard_map/dot_general | solution.py:33
  114.6 1.4 pad_maximum_fusion
  115.9 31.8 %psum.21 = f32[2]{0:T(128)S(1)} all-reduce(f32[2]{0:T(128)S(1)} %pad_maximum_fusion), channel_id=1, replica_groups=mesh['nodes'=16] {'nodes'}, use_global_device_ids=true, to_apply=%region_5.6 | all-reduce | flops 2 | bytes 16 | tf_op jit(solution)/shard_map/psum | solution.py:38
  148.4 0.6 convert_divide_fusion
  149.1 15.4 %fusion.1 = f32[16384,47]{0,1:T(8,128)} fusion(bf16[1024,16384]{1,0:T(8,128)(2,1)} %param.7, f32[16384]{0:T(1024)S(1)} %bitcast.71, f32[47,1024]{1,0:T(8,128)S(1)} %get-tuple-element.15, f32[1024]{0:T(1024)S(1)} %convert_divide_fusion, f32[1024]{0:T(1024)S(1)} %get-tuple-element.9, s32[1024]{0:T(1024)S(1)} %copy-done.3), kind=kOutput, calls=%fused_computation.3 | convolution fusion | flops 1578117120 | bytes 36904960 | tf_op jit(solution)/shard_map/dot_general | solution.py:19
  164.8 55.2 %reduce-scatter.3.cloned.1.call-done = f32[1024,47]{0,1:T(8,128)} async-done(((f32[16384,47]{0,1:T(8,128)}), f32[1024,47]{0,1:T(8,128)}) %reduce-scatter.3.cloned.1.call-update) | async-done | bytes 192528 | tf_op jit(solution)/shard_map/reduce_scatter | solution.py:21
  220.0 16.6 %fusion = f32[16384,128]{0,1:T(8,128)} fusion(bf16[1024,16384]{1,0:T(8,128)(2,1)} %param.7, f32[16384]{0:T(1024)S(1)} %bitcast.72, f32[128,1024]{1,0:T(8,128)S(1)} %fusion.33, f32[1024,47]{0,1:T(8,128)} %reduce-scatter.3.cloned.1.call-done, f32[128,47]{0,1:T(8,128)S(1)} %copy-done.2), kind=kOutput, calls=%fused_computation.1 | convolution fusion | flops 4309832704 | bytes 42749440 | tf_op jit(solution)/shard_map/dot_general | solution.py:19
  236.7 0.9 copy-done.1
  237.5 0.8 fusion.16
  238.3 91.2 %reduce-scatter.5.cloned.1.call-done = f32[1024,128]{0,1:T(8,128)} async-done(((f32[16384,128]{0,1:T(8,128)}), f32[1024,128]{0,1:T(8,128)}) %reduce-scatter.5.cloned.1.call-update) | async-done | bytes 524304 | tf_op jit(solution)/shard_map/reduce_scatter | solution.py:21
  329.5 1.9 convolution_bitcast_fusion
  332.7 65.4 %all-reduce.3.cloned.1.call-done = (f32[100,128]{1,0:T(8,128)}, f32[128,47]{0,1:T(8,128)}) async-done(((f32[100,128]{1,0:T(8,128)}, f32[128,47]{0,1:T(8,128)}), (f32[100,128]{1,0:T(8,128)}, f32[128,47]{0,1:T(8,128)})) %all-reduce.3.cloned.1.call-update) | async-done | bytes 75280 | tf_op jit(solution)/shard_map/psum | solution.py:48
  398.1 1.4 copy.15
  399.5 1.3 copy.16
  (26 shorter events, 2.2 us)
Async XLA Ops:
  7.2 0.9 copy-start
  7.2 40.9 %all-gather.5.cloned.1.call-start = ((), (), s32[]{:S(2)}) async-start(), calls=%async_computation.4 | async-start | bytes 4456448 | tf_op jit(solution)/shard_map/all_gather | solution.py:12
  9.9 85.2 %all-gather.7.cloned.1.call-start = ((), (), s32[]{:S(2)}) async-start(), calls=%async_computation.5 | async-start | bytes 1671168 | tf_op jit(solution)/shard_map/all_gather | solution.py:12
  50.6 16.1 %copy-start.2 = (f32[128,47]{0,1:T(8,128)S(1)}, f32[128,47]{0,1:T(8,128)}, u32[]{:S(2)}) copy-start(f32[128,47]{0,1:T(8,128)} %param.10) | copy-start | bytes 72196
  67.6 152.4 %reduce-scatter.3.cloned.1.call-start = ((), (), s32[]{:S(2)}) async-start(), calls=%async_computation.2 | async-start | bytes 3342336 | tf_op jit(solution)/shard_map/reduce_scatter | solution.py:21
  98.6 15.2 %copy-start.3 = (s32[1024]{0:T(1024)S(1)}, s32[1024]{0:T(1024)}, u32[]{:S(2)}) copy-start(s32[1024]{0:T(1024)} %param.11) | copy-start | bytes 12292
  98.7 15.3 %copy-start.4 = (s32[1024]{0:T(1024)S(1)}, s32[1024]{0:T(1024)}, u32[]{:S(2)}) copy-start(s32[1024]{0:T(1024)} %param.12) | copy-start | bytes 12292
  164.5 165.0 %reduce-scatter.5.cloned.1.call-start = ((), (), s32[]{:S(2)}) async-start(), calls=%async_computation.3 | async-start | bytes 8912896 | tf_op jit(solution)/shard_map/reduce_scatter | solution.py:21
  236.6 0.9 copy-start.1
  236.6 161.5 %all-reduce.3.cloned.1.call-start = ((), (), s32[]{:S(2)}) async-start(), calls=%async_computation.6 | async-start | bytes 155648 | tf_op jit(solution)/shard_map/psum | solution.py:48
Sparse Core Ops, SparseCore 0:
  10.2 37.8 all-gather.4
  67.7 27.2 all-gather.6
  164.6 55.2 reduce-scatter.2
  236.7 92.7 reduce-scatter.4
  334.4 63.6 all-reduce.2
where the time goes:
time: 409 us
  waiting for transfers between devices  277 us (68%)
  matrix products  68.6 us (17%)
  blocking collectives  31.8 us (8%)
  between operations  16.3 us (4%)
  local copies, waits for them, and re-layouts  8.64 us (2%)
  other arithmetic  6.09 us (1%)
    reduce_scatter x2, waiting for transfers between devices, transpose_product_scatter(): lax.psum_scatter(contrib.reshape(-1, width), AXIS_NAME, scatter_dimension...  146 us
    psum x1, waiting for transfers between devices, device_step(): lax.psum(lax.dot_general(feat_rows, grad_proj_one, ROW_CONTRACT, preferre...  65.4 us
    all_gather x2, waiting for transfers between devices, gather_masked(): gathered = lax.all_gather(local_vals, AXIS_NAME, axis=0, tiled=False)  64.8 us
    dot_general x2, matrix products, transpose_product_scatter(): lax.dot_general(adj_rows, local_grad, ROW_CONTRACT, preferred_element_typ...  32 us
    psum x1, blocking collectives, device_step(): lax.psum(jnp.stack([jnp.sum(label_weight), jnp.sum(label_weight * (log_no...  31.8 us
    dot_general x1, matrix products, device_step(): jnp.dot(adj_rows, gather_masked(proj_one, mask_row), preferred_element_ty...  16.1 us
    dot_general x1, matrix products, device_step(): jnp.dot(adj_rows, gather_masked(proj_two, mask_row), preferred_element_ty...  15.2 us
  transfers between devices with their start and end apart: 5, of which 5 were waited for; matrix products, arithmetic and copies ran while one was open for 0% of the time, Pallas kernels for 0%

commit v1 on v0

v1 whole, which is shorter than its diff:
```python
import jax
import jax.numpy as jnp
from jax import lax
from jax.experimental import pallas as pl
from jax.experimental.pallas import tpu as pltpu
from jax.sharding import PartitionSpec as P

AXIS_NAME = 'nodes'
MESH = pl.DeviceIdType.MESH
F32, BF16 = jnp.float32, jnp.bfloat16
BLK = 1024
NB = 16
F_IN, F_PAD, MASK_ROW = 100, 112, 100
HID = 128
CLS, CLS_PAD = 47, 48
QS = [0, 1, 2, 4, 3, 5, 6, 7]
QI = {q: i for i, q in enumerate(QS)}
ORDERS = [(1, 2, 4), (2, 4, 1), (4, 1, 2)]
X_CHUNKS = [(0, 48), (48, 32), (80, 32)]
Y_CHUNKS = [(0, 16), (16, 16), (32, 16)]
D1_CHUNKS = [(0, 48), (48, 40), (88, 40)]
AR_ROWS = 80


def dot_last(lhs, rhs):
    return lax.dot_general(lhs, rhs, (((1,), (1,)), ((), ())), preferred_element_type=F32)


def dot_first(lhs, rhs):
    return lax.dot_general(lhs, rhs, (((0,), (0,)), ((), ())), preferred_element_type=F32)


def step_kernel(adj_hbm, x_hbm, wh_ref, wot_ref, lab_ref, msk_ref, bm_ref, gwh_ref, gwot_ref, loss_ref,
                adj, xall, yall, z1, z1t, z2, hid, gt, et, con, part2, part1, rb2, rb1, whs, wos, macc, lossv, gwhs, gwos, ar, arp, ars, arb, arg,
                a_sem, x_sem, ici_send, d2d_send, ag1_recv, ag1_d2d, ag2_recv, ag2_d2d, rs2_recv, rs2_d2d, rs1_recv, rs1_d2d,
                ar_send, ar_recv):
    me = lax.axis_index(AXIS_NAME)
    coords = [me % 2, (me // 2) % 2, (me // 4) % 2, me // 8]

    def dev(rel):
        total = 0
        for bit in range(4):
            total = total + ((coords[bit] + ((rel >> bit) & 1)) % 2) * (1 << bit)
        return total

    def rel_of(slot):
        return 2 * QS[slot // 2] + slot % 2

    def rcopy(src, dst, send_sem, recv_sem, rel):
        return pltpu.make_async_remote_copy(src_ref=src, dst_ref=dst, send_sem=send_sem, recv_sem=recv_sem,
                                            device_id=(dev(rel),), device_id_type=MESH)

    def a_copy(slot, blk=0):
        return pltpu.make_async_copy(adj_hbm.at[:, pl.ds(pl.multiple_of(blk * BLK, BLK), BLK)], adj.at[slot], a_sem.at[slot])

    a_order = [0, 1, 2, 4, 6, 3, 5, 7, 8, 10, 12, 9, 11, 13, 14, 15]

    def start_a(lo, hi):
        for slot in a_order[lo:hi]:
            a_copy(slot, dev(rel_of(slot))).start()

    x_copy = pltpu.make_async_copy(x_hbm, xall.at[0], x_sem)
    x_copy.start()
    start_a(0, 6)
    barrier = pltpu.get_barrier_semaphore()
    peers = [1] + [2 * q for q in range(1, 8)]
    for rel in peers:
        pl.semaphore_signal(barrier, inc=1, device_id=(dev(rel),), device_id_type=MESH)

    whs[...] = jnp.zeros_like(whs)
    whs[0:F_IN, :] = wh_ref[...].astype(BF16)
    wos[...] = jnp.zeros_like(wos)
    wos[0:CLS, :] = wot_ref[...].astype(BF16)
    macc[...] = jnp.zeros_like(macc)
    x_copy.wait()
    pl.semaphore_wait(barrier, len(peers))

    def mask_of(slot):
        if isinstance(slot, int):
            return bm_ref[me, dev(rel_of(slot))]
        i = slot // 2
        c = slot % 2
        bits = []
        for bit in (1, 2, 4):
            b = 0
            for pos, q in enumerate(QS):
                if q & bit:
                    d = (i - pos) * (i - pos)
                    b = b + 1 // (1 + d)
            bits.append(b)
        total = ((coords[0] + c) % 2)
        for n, b in enumerate(bits):
            total = total + ((coords[n + 1] + b) % 2) * (2 << n)
        return bm_ref[me, total]


    def ag_ops(buf, chunks, recv, recv_d2d):
        def ici(src_q, dim, k):
            dst_q = src_q ^ dim
            lo, n = chunks[k]
            idx = k * 7 + QI[dst_q] - 1
            return rcopy(buf.at[2 * QI[src_q], pl.ds(lo, n), :], buf.at[2 * QI[dst_q], pl.ds(lo, n), :],
                         ici_send.at[idx], recv.at[idx], 2 * dim)

        def d2d(q_idx):
            return rcopy(buf.at[2 * q_idx], buf.at[2 * q_idx + 1], d2d_send.at[q_idx], recv_d2d.at[q_idx], 1)

        def recv_wait(dst_q, k):
            o = ORDERS[k]
            dim = max((d for d in o if dst_q & d), key=o.index)
            ici(dst_q ^ dim, dim, k).wait_recv()

        def send_own():
            for j in range(3):
                for k in range(3):
                    ici(0, ORDERS[k][j], k).start()
            d2d(0).start()

        def near():
            for k in range(3):
                a, b, c = ORDERS[k]
                recv_wait(a, k)
                ici(a, b, k).start()
                ici(a, c, k).start()
            for k in range(3):
                a, b, c = ORDERS[k]
                recv_wait(b, k)
                ici(b, c, k).start()

        def near_last():
            for k in range(3):
                recv_wait(ORDERS[k][2], k)
            for q in (1, 2, 4):
                d2d(QI[q]).start()

        def mid():
            for k in range(3):
                a, b, c = ORDERS[k]
                recv_wait(a | b, k)
                ici(a | b, c, k).start()

        def mid_last():
            for k in range(3):
                recv_wait(ORDERS[k][0] | ORDERS[k][2], k)
            for k in range(3):
                recv_wait(ORDERS[k][1] | ORDERS[k][2], k)
            for q in (3, 5, 6):
                d2d(QI[q]).start()

        def far():
            for k in range(3):
                recv_wait(7, k)
            d2d(QI[7]).start()

        def wait_sends():
            for k in range(3):
                o = ORDERS[k]
                for q in range(1, 8):
                    dim = max((d for d in o if q & d), key=o.index)
                    ici(q ^ dim, dim, k).wait_send()
            for i in range(8):
                d2d(i).wait_send()

        return dict(d2d=d2d, send_own=send_own, near=near, near_last=near_last, mid=mid, mid_last=mid_last, far=far,
                    wait_sends=wait_sends)

    def forward_pass(ag, compute, first):
        compute(0)
        ag['near']()
        ag['d2d'](0).wait_recv()
        compute(1)
        ag['near_last']()

        def group(g, carry):
            base = 2 + (g % 2) + 6 * (g // 2)

            @pl.when(g == 1)
            def _():
                ag['mid']()
                for q in (1, 2, 4):
                    ag['d2d'](QI[q]).wait_recv()

            @pl.when(g == 2)
            def _():
                ag['mid_last']()

            @pl.when(g == 3)
            def _():
                ag['far']()
                for q in (3, 5, 6):
                    ag['d2d'](QI[q]).wait_recv()

            for j in range(3):
                compute(base + 2 * j)
            return carry

        lax.fori_loop(0, 4, group, 0)
        compute(14)
        ag['d2d'](7).wait_recv()
        compute(15)
        ag['wait_sends']()

    ag1 = ag_ops(xall, X_CHUNKS, ag1_recv, ag1_d2d)
    ag1['send_own']()
    start_a(6, 16)

    def compute1(slot):
        a_copy(slot).wait()
        xt = xall[slot]
        macc[...] += xall[slot, MASK_ROW - 4:MASK_ROW + 12, :].astype(F32)
        yt = (dot_first(whs[...], xt).astype(BF16).astype(F32) * mask_of(slot).astype(F32)).astype(BF16)
        prod = dot_last(adj[slot], yt)
        if isinstance(slot, int) and slot == 0:
            z1[...] = prod
        else:
            z1[...] += prod

    forward_pass(ag1, compute1, True)
    label_count = jnp.sum(macc[4:5, :])

    hid[...] = jnp.maximum(z1[...], 0.0).astype(BF16)
    yall[0] = dot_last(wos[...], hid[...]).astype(BF16)
    ag2 = ag_ops(yall, Y_CHUNKS, ag2_recv, ag2_d2d)
    z1t[...] = jnp.transpose(z1[...])
    ag2['send_own']()

    def compute2(slot):
        yt = (yall[slot].astype(F32) * mask_of(slot).astype(F32)).astype(BF16)
        prod = dot_last(adj[slot], yt)
        if isinstance(slot, int) and slot == 0:
            z2[...] = prod
        else:
            z2[...] += prod

    forward_pass(ag2, compute2, False)

    zt = jnp.transpose(z2[...])
    cls_id = lax.broadcasted_iota(jnp.int32, (CLS_PAD, BLK), 0)
    valid = cls_id < CLS
    top = jnp.max(jnp.where(valid, zt, -jnp.inf), axis=0, keepdims=True)
    expz = jnp.where(valid, jnp.exp(zt - top), 0.0)
    log_norm = jnp.log(jnp.sum(expz, axis=0, keepdims=True)) + top
    one_hot = cls_id == lab_ref[...]
    picked = jnp.sum(jnp.where(one_hot, zt, 0.0), axis=0, keepdims=True)
    weight = msk_ref[...].astype(F32)
    loss_terms = weight * (log_norm - picked)
    acc = loss_terms[:, 0:128]
    for n in range(1, BLK // 128):
        acc = acc + loss_terms[:, 128 * n:128 * (n + 1)]
    lossv[...] = acc
    prob = jnp.exp(zt - log_norm)
    grad = (prob - one_hot.astype(F32)) * (weight / label_count)
    gt[...] = jnp.where(valid, grad, 0.0).astype(BF16)


    def reduce_pass(lhs_ref, rows, chunks, part, rb, recv, recv_d2d):
        def dim_of(q, k):
            return next(d for d in reversed(ORDERS[k]) if q & d)

        def ici(q, k):
            lo, n = chunks[k]
            idx = k * 7 + QI[q] - 1
            return rcopy(con.at[2 * QI[q], pl.ds(lo, n), :], rb.at[QI[q] - 1, pl.ds(lo, n), :], ici_send.at[idx],
                         recv.at[idx], 2 * dim_of(q, k))

        def d2d(i):
            return rcopy(con.at[2 * i + 1, pl.ds(0, rows), :], part.at[i], d2d_send.at[i], recv_d2d.at[i], 1)

        def sources(q, k):
            out = []
            for d in reversed(ORDERS[k]):
                if q & d:
                    break
                out.append(q ^ d)
            return out

        def compute(slot):
            lhs = (lhs_ref[...].astype(F32) * mask_of(slot).astype(F32)).astype(BF16)
            con[slot, 0:rows, :] = jnp.dot(lhs, adj[slot], preferred_element_type=F32)

        waiting = {(q, k): set(sources(q, k)) for q in range(8) for k in range(3)}

        def pair_sum(q):
            i = QI[q]
            d2d(i).wait_recv()
            con[2 * i, 0:rows, :] += part[i]
            for k in range(3):
                if q and not waiting[q, k]:
                    ici(q, k).start()

        def take(src, k):
            d = dim_of(src, k)
            q = src ^ d
            lo, n = chunks[k]
            ici(src, k).wait_recv()
            con[2 * QI[q], lo:lo + n, :] += rb[QI[src] - 1, lo:lo + n, :]
            waiting[q, k].discard(src)
            if q and not waiting[q, k]:
                ici(q, k).start()

        def body(n, carry):
            i = 7 - n
            compute(2 * i + 1)
            d2d(i).start()
            compute(2 * i)
            for m in range(1, 8):
                @pl.when(n == m)
                def _(m=m):
                    pair_sum(QS[8 - m])
            return carry

        lax.fori_loop(0, 8, body, 0)
        pair_sum(0)
        send_rank = {q: r for r, q in enumerate(reversed(QS))}
        todo = []
        for k in range(3):
            for src in range(1, 8):
                phase = list(reversed(ORDERS[k])).index(dim_of(src, k))
                todo.append((phase, send_rank[src], k, src))
        for phase, _, k, src in sorted(todo):
            take(src, k)
        for k in range(3):
            for q in range(1, 8):
                ici(q, k).wait_send()
        for i in range(8):
            d2d(i).wait_send()

    reduce_pass(gt, CLS_PAD, Y_CHUNKS, part2, rb2, rs2_recv, rs2_d2d)
    d2t = con[0, 0:CLS_PAD, :].astype(BF16)
    gwo = jnp.dot(d2t, hid[...], preferred_element_type=F32)
    et[...] = jnp.where(z1t[...] > 0, dot_first(wos[...], d2t), 0.0).astype(BF16)
    row_id = lax.broadcasted_iota(jnp.int32, (CLS_PAD, HID), 0)
    gwos[...] = jnp.where(row_id == CLS, lossv[...], gwo)

    reduce_pass(et, HID, D1_CHUNKS, part1, rb1, rs1_recv, rs1_d2d)
    d1t = con[0].astype(BF16)
    gwhs[...] = dot_last(xall[0], d1t)

    ar[0] = gwhs[0:AR_ROWS, :]
    ar[1, 0:24, :] = gwhs[AR_ROWS:104, :]
    ar[1, 24:72, :] = gwos[...]
    ar[1, 72:80, :] = jnp.zeros((8, HID), F32)
    core = coords[0]
    pair = rcopy(ar.at[1 - core], arp, ar_send.at[0], ar_recv.at[0], 1)
    pair.start()
    pair.wait()
    arg[0] = ar[core] + arp[...]
    sends = [rcopy(arg.at[0], arg.at[q], ar_send.at[q], ar_recv.at[q], 2 * q) for q in range(1, 8)]
    for q in (7, 6, 5, 3, 4, 2, 1):
        sends[q - 1].start()
    for cp in sends:
        cp.wait()
    total = ((arg[0] + arg[1]) + (arg[2] + arg[3])) + ((arg[4] + arg[5]) + (arg[6] + arg[7]))
    ars[...] = total
    back = rcopy(ars, arb, ar_send.at[8], ar_recv.at[8], 1)
    back.start()
    ar[core] = total
    back.wait()
    ar[1 - core] = arb[...]
    gwh_ref[0:AR_ROWS, :] = ar[0]
    gwh_ref[AR_ROWS:F_IN, :] = ar[1, 0:F_IN - AR_ROWS, :]
    gwot_ref[...] = ar[1, 24:24 + CLS, :]
    loss_ref[...] = jnp.sum(ar[1, 24 + CLS:24 + CLS_PAD, :], axis=1, keepdims=True) / label_count


def device_step(adj_rows, feat_rows, w_hidden, w_output, labels, train_mask, block_mask):
    mask_row = train_mask.astype(BF16)[None, :]
    x_ext = jnp.concatenate([feat_rows.T, mask_row, jnp.zeros((F_PAD - F_IN - 1, BLK), BF16)], axis=0)
    dma = pltpu.SemaphoreType.DMA
    vmem = pl.BlockSpec(memory_space=pltpu.VMEM)
    hbm = pl.BlockSpec(memory_space=pl.ANY)
    gwh, gwot, loss = pl.pallas_call(
        step_kernel,
        name='gcn_step',
        out_shape=(jax.ShapeDtypeStruct((F_IN, HID), F32), jax.ShapeDtypeStruct((CLS, HID), F32),
                   jax.ShapeDtypeStruct((1, 1), F32)),
        in_specs=[hbm, hbm, vmem, vmem, vmem, vmem, pl.BlockSpec(memory_space=pltpu.SMEM)],
        out_specs=(vmem, vmem, vmem),
        scratch_shapes=[
            pltpu.VMEM((NB, BLK, BLK), BF16),
            pltpu.VMEM((NB, F_PAD, BLK), BF16),
            pltpu.VMEM((NB, CLS_PAD, BLK), BF16),
            pltpu.VMEM((BLK, HID), F32),
            pltpu.VMEM((HID, BLK), F32),
            pltpu.VMEM((BLK, CLS_PAD), F32),
            pltpu.VMEM((BLK, HID), BF16),
            pltpu.VMEM((CLS_PAD, BLK), BF16),
            pltpu.VMEM((HID, BLK), BF16),
            pltpu.VMEM((NB, HID, BLK), F32),
            pltpu.VMEM((8, CLS_PAD, BLK), F32),
            pltpu.VMEM((8, HID, BLK), F32),
            pltpu.VMEM((7, CLS_PAD, BLK), F32),
            pltpu.VMEM((7, HID, BLK), F32),
            pltpu.VMEM((F_PAD, HID), BF16),
            pltpu.VMEM((CLS_PAD, HID), BF16),
            pltpu.VMEM((16, BLK), F32),
            pltpu.VMEM((1, 128), F32),
            pltpu.VMEM((F_PAD, HID), F32),
            pltpu.VMEM((CLS_PAD, HID), F32),
            pltpu.VMEM((2, AR_ROWS, HID), F32),
            pltpu.VMEM((AR_ROWS, HID), F32),
            pltpu.VMEM((AR_ROWS, HID), F32),
            pltpu.VMEM((AR_ROWS, HID), F32),
            pltpu.VMEM((8, AR_ROWS, HID), F32),
            dma((NB,)), dma, dma((21,)), dma((8,)),
            dma((21,)), dma((8,)), dma((21,)), dma((8,)), dma((21,)), dma((8,)), dma((21,)), dma((8,)),
            dma((9,)), dma((9,)),
        ],
        compiler_params=pltpu.CompilerParams(collective_id=0, has_side_effects=True, vmem_limit_bytes=67043328),
    )(adj_rows, x_ext, w_hidden, w_output.T, labels[None, :], train_mask[None, :], block_mask)
    return loss[0, 0], gwh, gwot.T


def solution(mesh):
    row_spec = P(AXIS_NAME, None)
    vec_spec = P(AXIS_NAME)
    return jax.shard_map(device_step, mesh=mesh, in_specs=(row_spec, row_spec, P(), P(), vec_spec, vec_spec, P()), out_specs=(P(), P(), P()), check_vma=False)
```

time: 409 us -> 115 us (0.28)
  waiting for transfers between devices: 277 us -> 0 us
  Pallas kernels: 0 us -> 107 us
  matrix products: 68.6 us -> 0 us
  blocking collectives: 31.8 us -> 0 us
  between operations: 16.3 us -> 2.33 us
  local copies, waits for them, and re-layouts: 8.64 us -> 2.87 us
    reduce_scatter x2 -> x0, waiting for transfers between devices: 146 us -> none  [transpose_product_scatter(): lax.psum_scatter(contrib.reshape(-1, width), AXIS_NAME, scatter_dimension...]
    pallas_call x0 -> x1, Pallas kernels: none -> 107 us  [device_step(): pl.pallas_call(step_kernel, name='gcn_step', out_shape=(jax.ShapeDtypeStr...]
    dot_general x8 -> x0, matrix products: 68.6 us -> none  [the longest x2 32 us: transpose_product_scatter(): lax.dot_general(adj_rows, local_grad, ROW_CONTRACT, preferred_element_typ...]
    psum x1 -> x0, waiting for transfers between devices: 65.4 us -> none  [device_step(): lax.psum(lax.dot_general(feat_rows, grad_proj_one, ROW_CONTRACT, preferre...]
    all_gather x2 -> x0, waiting for transfers between devices: 64.8 us -> none  [gather_masked(): gathered = lax.all_gather(local_vals, AXIS_NAME, axis=0, tiled=False)]
    psum x1 -> x0, blocking collectives: 31.8 us -> none  [device_step(): lax.psum(jnp.stack([jnp.sum(label_weight), jnp.sum(label_weight * (log_no...]
    unnamed x17 -> x2, local copies, waits for them, and re-layouts: 8.03 us -> 2.78 us
  transfers between devices with their start and end apart: 5 -> 0, of which waited for: 5 -> 0; matrix products, arithmetic and copies ran while one was open for 0% -> 0% of each run, Pallas kernels for 0% -> 0%
where the time goes in v1:
time: 115 us
  Pallas kernels  107 us (93%)
  local copies, waits for them, and re-layouts  2.87 us (2%)
  other arithmetic  2.41 us (2%)
  between operations  2.33 us (2%)
    pallas_call x1, Pallas kernels, device_step(): pl.pallas_call(step_kernel, name='gcn_step', out_shape=(jax.ShapeDtypeStr...  107 us
    unnamed x2, local copies, waits for them, and re-layouts  2.78 us

profile of v1, /device:TPU:0, one launch (start us, length us, event | category | flops | bytes accessed | tf_op | source)
XLA Modules:
  0.0 114.6 jit_solution(14821270146227378852)
XLA Ops:
  0.6 0.1 pad.2.clone
  0.7 0.7 convert_element_type.3
  1.4 1.7 %maximum_maximum_fusion.x_hbm = bf16[112,1024]{1,0:T(8,128)(2,1)} fusion(bf16[1,1024]{1,0:T(2,128)(2,1)S(1)} %broadcast_in_dim.12, bf16[100,1024]{1,0:T(8,128)(2,1)} %bitcast.6, bf16[112]{0:T(256)(128)(2,1)S(1)} %pad.2.clone), kind=kLoop, calls=%fused_computation | loop fusion | flops 688128 | bytes 436448 | tf_op jit(solution)/shard_map/concatenate | solution.py:368
  3.1 107.0 %gcn_step.1 = (f32[100,128]{1,0:T(8,128)}, f32[47,128]{1,0:T(8,128)}, f32[1,1]{1,0:T(1,128)}) custom-call(bf16[1024,16384]{1,0:T(8,128)(2,1)} %adj_hbm.1, bf16[112,1024]{1,0:T(8,128)(2,1)} %maximum_maximum_fusion.x_hbm, f32[100,128]{1,0:T(8,128)} %wh_ref.1, f32[47,128]{1,0:T(8,128)} %bitcast.8, s32[1,1024]{1,0:T(1,128)} %bitcast.10, s32[1,1024]{1,0:T(1,128)} %bitcast.9, ...), custom_call_target="tpu_custom_call" | custom-call | tf_op jit(solution)/shard_map/gcn_step/pallas_call | solution.py:372
  110.7 1.4 %copy.14 = f32[100,128]{1,0:T(8,128)} copy(f32[100,128]{1,0:T(8,128)} %get-tuple-element.13) | data formatting | bytes 102400
  112.1 1.3 %copy.15 = f32[128,47]{0,1:T(8,128)} copy(f32[128,47]{0,1:T(8,128)} %bitcast.7) | data formatting | bytes 48128
  (2 shorter events, 0.0 us)

commit v2 on v1

--- a/solution.py
+++ b/solution.py
@@ -10,16 +10,17 @@
 F32, BF16 = jnp.float32, jnp.bfloat16
 BLK = 1024
 NB = 16
-F_IN, F_PAD, MASK_ROW = 100, 112, 100
+F_IN, F_PAD = 100, 104
 HID = 128
 CLS, CLS_PAD = 47, 48
 QS = [0, 1, 2, 4, 3, 5, 6, 7]
 QI = {q: i for i, q in enumerate(QS)}
 ORDERS = [(1, 2, 4), (2, 4, 1), (4, 1, 2)]
-X_CHUNKS = [(0, 48), (48, 32), (80, 32)]
+X_CHUNKS = [(0, 40), (40, 32), (72, 32)]
 Y_CHUNKS = [(0, 16), (16, 16), (32, 16)]
 D1_CHUNKS = [(0, 48), (48, 40), (88, 40)]
-AR_ROWS = 80
+GWO_HALF, GWH_HALF = 24, 56
+M_TILE = 256
 
 
 def dot_last(lhs, rhs):
@@ -30,10 +31,11 @@
     return lax.dot_general(lhs, rhs, (((0,), (0,)), ((), ())), preferred_element_type=F32)
 
 
-def step_kernel(adj_hbm, x_hbm, wh_ref, wot_ref, lab_ref, msk_ref, bm_ref, gwh_ref, gwot_ref, loss_ref,
-                adj, xall, yall, z1, z1t, z2, hid, gt, et, con, part2, part1, rb2, rb1, whs, wos, macc, lossv, gwhs, gwos, ar, arp, ars, arb, arg,
-                a_sem, x_sem, ici_send, d2d_send, ag1_recv, ag1_d2d, ag2_recv, ag2_d2d, rs2_recv, rs2_d2d, rs1_recv, rs1_d2d,
-                ar_send, ar_recv):
+def step_kernel(adj_hbm, x_ref, wh_ref, wot_ref, lab_ref, msk_ref, bm_ref, gwh_ref, gwot_ref, loss_ref,
+                adj, xall, yall, y1b, z1, z1t, z2, hid, gt, et, con, part2, part1, rb2, rb1, whs, wos, macc, lossv,
+                gwos, gwop, gwor, gwog, gwof, gwhs, gwhp, gwhr, gwhg, gwhf,
+                a_sem, ici_send, d2d_send, recv_a, d2d_a, recv_b, d2d_b,
+                gwo_send, gwo_recv, gwh_send, gwh_recv):
     me = lax.axis_index(AXIS_NAME)
     coords = [me % 2, (me // 2) % 2, (me // 4) % 2, me // 8]
 
@@ -59,20 +61,21 @@
         for slot in a_order[lo:hi]:
             a_copy(slot, dev(rel_of(slot))).start()
 
-    x_copy = pltpu.make_async_copy(x_hbm, xall.at[0], x_sem)
-    x_copy.start()
     start_a(0, 6)
     barrier = pltpu.get_barrier_semaphore()
     peers = [1] + [2 * q for q in range(1, 8)]
     for rel in peers:
         pl.semaphore_signal(barrier, inc=1, device_id=(dev(rel),), device_id_type=MESH)
 
+    xall[0, 0:F_PAD - 8, :] = x_ref[0:F_PAD - 8, :]
+    xall[0, F_PAD - 8:F_PAD, :] = jnp.concatenate([x_ref[F_PAD - 8:F_IN, :], jnp.zeros((F_PAD - F_IN, BLK), BF16)], axis=0)
     whs[...] = jnp.zeros_like(whs)
     whs[0:F_IN, :] = wh_ref[...].astype(BF16)
     wos[...] = jnp.zeros_like(wos)
     wos[0:CLS, :] = wot_ref[...].astype(BF16)
     macc[...] = jnp.zeros_like(macc)
-    x_copy.wait()
+    z1[...] = jnp.zeros_like(z1)
+    z2[...] = jnp.zeros_like(z2)
     pl.semaphore_wait(barrier, len(peers))
 
     def mask_of(slot):
@@ -164,11 +167,11 @@
         return dict(d2d=d2d, send_own=send_own, near=near, near_last=near_last, mid=mid, mid_last=mid_last, far=far,
                     wait_sends=wait_sends)
 
-    def forward_pass(ag, compute, first):
-        compute(0)
+    def forward_pass(ag, compute):
+        compute([0])
         ag['near']()
         ag['d2d'](0).wait_recv()
-        compute(1)
+        compute([1])
         ag['near_last']()
 
         def group(g, carry):
@@ -190,59 +193,61 @@
                 for q in (3, 5, 6):
                     ag['d2d'](QI[q]).wait_recv()
 
-            for j in range(3):
-                compute(base + 2 * j)
+            compute([base, base + 2, base + 4])
             return carry
 
         lax.fori_loop(0, 4, group, 0)
-        compute(14)
+        compute([14])
         ag['d2d'](7).wait_recv()
-        compute(15)
+        compute([15])
         ag['wait_sends']()
 
-    ag1 = ag_ops(xall, X_CHUNKS, ag1_recv, ag1_d2d)
+    ag1 = ag_ops(xall, X_CHUNKS, recv_a, d2d_a)
     ag1['send_own']()
     start_a(6, 16)
 
-    def compute1(slot):
-        a_copy(slot).wait()
-        xt = xall[slot]
-        macc[...] += xall[slot, MASK_ROW - 4:MASK_ROW + 12, :].astype(F32)
-        yt = (dot_first(whs[...], xt).astype(BF16).astype(F32) * mask_of(slot).astype(F32)).astype(BF16)
-        prod = dot_last(adj[slot], yt)
-        if isinstance(slot, int) and slot == 0:
-            z1[...] = prod
-        else:
-            z1[...] += prod
-
-    forward_pass(ag1, compute1, True)
-    label_count = jnp.sum(macc[4:5, :])
+    def accumulate(out, slots, blocks):
+        for lo in range(0, BLK, M_TILE):
+            acc = out[lo:lo + M_TILE, :]
+            for slot, block in zip(slots, blocks):
+                acc = acc + dot_last(adj[slot, lo:lo + M_TILE, :], block)
+            out[lo:lo + M_TILE, :] = acc
+
+    def compute1(slots):
+        for slot in slots:
+            a_copy(slot).wait()
+        for j, slot in enumerate(slots):
+            yt = dot_first(whs[...], xall[slot]).astype(BF16)
+            y1b[j] = (yt.astype(F32) * mask_of(slot).astype(F32)).astype(BF16)
+        accumulate(z1, slots, [y1b[j] for j in range(len(slots))])
+
+    forward_pass(ag1, compute1)
 
     hid[...] = jnp.maximum(z1[...], 0.0).astype(BF16)
-    yall[0] = dot_last(wos[...], hid[...]).astype(BF16)
-    ag2 = ag_ops(yall, Y_CHUNKS, ag2_recv, ag2_d2d)
+    cls_id = lax.broadcasted_iota(jnp.int32, (CLS_PAD, BLK), 0)
+    weight = msk_ref[...].astype(F32)
+    yall[0] = jnp.where(cls_id == CLS, weight, dot_last(wos[...], hid[...])).astype(BF16)
+    ag2 = ag_ops(yall, Y_CHUNKS, recv_b, d2d_b)
+    ag2['send_own']()
     z1t[...] = jnp.transpose(z1[...])
-    ag2['send_own']()
-
-    def compute2(slot):
-        yt = (yall[slot].astype(F32) * mask_of(slot).astype(F32)).astype(BF16)
-        prod = dot_last(adj[slot], yt)
-        if isinstance(slot, int) and slot == 0:
-            z2[...] = prod
-        else:
-            z2[...] += prod
-
-    forward_pass(ag2, compute2, False)
+
+    def compute2(slots):
+        blocks = []
+        for slot in slots:
+            macc[...] += yall[slot, CLS_PAD - 16:CLS_PAD, :].astype(F32)
+            blocks.append((yall[slot].astype(F32) * mask_of(slot).astype(F32)).astype(BF16))
+        accumulate(z2, slots, blocks)
+
+    forward_pass(ag2, compute2)
+    label_count = jnp.sum(macc[15:16, :])
 
     zt = jnp.transpose(z2[...])
-    cls_id = lax.broadcasted_iota(jnp.int32, (CLS_PAD, BLK), 0)
     valid = cls_id < CLS
     top = jnp.max(jnp.where(valid, zt, -jnp.inf), axis=0, keepdims=True)
     expz = jnp.where(valid, jnp.exp(zt - top), 0.0)
     log_norm = jnp.log(jnp.sum(expz, axis=0, keepdims=True)) + top
     one_hot = cls_id == lab_ref[...]
     picked = jnp.sum(jnp.where(one_hot, zt, 0.0), axis=0, keepdims=True)
-    weight = msk_ref[...].astype(F32)
     loss_terms = weight * (log_norm - picked)
     acc = loss_terms[:, 0:128]
     for n in range(1, BLK // 128):
@@ -253,7 +258,7 @@
     gt[...] = jnp.where(valid, grad, 0.0).astype(BF16)
 
 
-    def reduce_pass(lhs_ref, rows, chunks, part, rb, recv, recv_d2d):
+    def reduce_pass(lhs_ref, rows, chunks, part, rb, recv, recv_d2d, early, hooks):
         def dim_of(q, k):
             return next(d for d in reversed(ORDERS[k]) if q & d)
 
@@ -303,69 +308,117 @@
             compute(2 * i + 1)
             d2d(i).start()
             compute(2 * i)
-            for m in range(1, 8):
+            for m in range(8):
                 @pl.when(n == m)
                 def _(m=m):
-                    pair_sum(QS[8 - m])
+                    if m:
+                        pair_sum(QS[8 - m])
+                    for r in early.get(m, ()):
+                        take_rank(r)
+                    for hook in hooks.get(m, ()):
+                        hook()
             return carry
 
+        rank = {q: r for r, q in enumerate(reversed(QS))}
+        taken = set()
+
+        def sources_of(k, phase):
+            d = ORDERS[k][2 - phase]
+            later = [e for e in ORDERS[k][3 - phase:]]
+            return sorted((q for q in range(1, 8) if q & d and not any(q & e for e in later)), key=rank.get)
+
+        def take_rank(r, phase=0):
+            for k in range(3):
+                take(sources_of(k, phase)[r], k)
+                taken.add((phase, r))
+
         lax.fori_loop(0, 8, body, 0)
-        pair_sum(0)
-        send_rank = {q: r for r, q in enumerate(reversed(QS))}
-        todo = []
-        for k in range(3):
-            for src in range(1, 8):
-                phase = list(reversed(ORDERS[k])).index(dim_of(src, k))
-                todo.append((phase, send_rank[src], k, src))
-        for phase, _, k, src in sorted(todo):
-            take(src, k)
+        for r in range(4):
+            if (0, r) not in taken:
+                take_rank(r)
+            if r == 2:
+                for hook in hooks.get('mid', ()):
+                    hook()
+                pair_sum(0)
+        take_rank(0, 1)
+        take_rank(1, 1)
+        for hook in hooks.get('late', ()):
+            hook()
+        take_rank(0, 2)
         for k in range(3):
             for q in range(1, 8):
                 ici(q, k).wait_send()
         for i in range(8):
             d2d(i).wait_send()
 
-    reduce_pass(gt, CLS_PAD, Y_CHUNKS, part2, rb2, rs2_recv, rs2_d2d)
+    reduce_pass(gt, CLS_PAD, Y_CHUNKS, part2, rb2, recv_a, d2d_a, {6: [0], 7: [1]}, {})
     d2t = con[0, 0:CLS_PAD, :].astype(BF16)
     gwo = jnp.dot(d2t, hid[...], preferred_element_type=F32)
     et[...] = jnp.where(z1t[...] > 0, dot_first(wos[...], d2t), 0.0).astype(BF16)
     row_id = lax.broadcasted_iota(jnp.int32, (CLS_PAD, HID), 0)
     gwos[...] = jnp.where(row_id == CLS, lossv[...], gwo)
 
-    reduce_pass(et, HID, D1_CHUNKS, part1, rb1, rs1_recv, rs1_d2d)
-    d1t = con[0].astype(BF16)
-    gwhs[...] = dot_last(xall[0], d1t)
-
-    ar[0] = gwhs[0:AR_ROWS, :]
-    ar[1, 0:24, :] = gwhs[AR_ROWS:104, :]
-    ar[1, 24:72, :] = gwos[...]
-    ar[1, 72:80, :] = jnp.zeros((8, HID), F32)
     core = coords[0]
-    pair = rcopy(ar.at[1 - core], arp, ar_send.at[0], ar_recv.at[0], 1)
-    pair.start()
-    pair.wait()
-    arg[0] = ar[core] + arp[...]
-    sends = [rcopy(arg.at[0], arg.at[q], ar_send.at[q], ar_recv.at[q], 2 * q) for q in range(1, 8)]
-    for q in (7, 6, 5, 3, 4, 2, 1):
-        sends[q - 1].start()
-    for cp in sends:
-        cp.wait()
-    total = ((arg[0] + arg[1]) + (arg[2] + arg[3])) + ((arg[4] + arg[5]) + (arg[6] + arg[7]))
-    ars[...] = total
-    back = rcopy(ars, arb, ar_send.at[8], ar_recv.at[8], 1)
-    back.start()
-    ar[core] = total
-    back.wait()
-    ar[1 - core] = arb[...]
-    gwh_ref[0:AR_ROWS, :] = ar[0]
-    gwh_ref[AR_ROWS:F_IN, :] = ar[1, 0:F_IN - AR_ROWS, :]
-    gwot_ref[...] = ar[1, 24:24 + CLS, :]
-    loss_ref[...] = jnp.sum(ar[1, 24 + CLS:24 + CLS_PAD, :], axis=1, keepdims=True) / label_count
+
+    def all_sum(rows, total_rows, src, halves, other, own, gathered, final, send, recv):
+        def prepare():
+            halves[0] = src[0:rows, :]
+            halves[1, 0:total_rows - rows, :] = src[rows:total_rows, :]
+            if total_rows < 2 * rows:
+                halves[1, total_rows - rows:rows, :] = jnp.zeros((2 * rows - total_rows, HID), F32)
+
+        pair = rcopy(halves.at[1 - core], other, send.at[0], recv.at[0], 1)
+        sends = [rcopy(gathered.at[0], gathered.at[q], send.at[q], recv.at[q], 2 * q) for q in range(1, 8)]
+        back = rcopy(own, final, send.at[8], recv.at[8], 1)
+
+        def start():
+            prepare()
+            pair.start()
+
+        def spread():
+            pair.wait()
+            gathered[0] = halves[core] + other[...]
+            for q in (7, 6, 5, 3, 4, 2, 1):
+                sends[q - 1].start()
+
+        def collect():
+            for cp in sends:
+                cp.wait()
+            g = gathered
+            own[...] = ((g[0] + g[1]) + (g[2] + g[3])) + ((g[4] + g[5]) + (g[6] + g[7]))
+            back.start()
+
+        def finish():
+            halves[core] = own[...]
+            back.wait()
+            halves[1 - core] = final[...]
+
+        return start, spread, collect, finish
+
+    gwo_start, gwo_spread, gwo_collect, gwo_finish = all_sum(GWO_HALF, CLS_PAD, gwos, gwop, gwof.at[0], gwor, gwog,
+                                                             gwof.at[1], gwo_send, gwo_recv)
+    gwh_start, gwh_spread, gwh_collect, gwh_finish = all_sum(GWH_HALF, F_PAD, gwhs, gwhp, gwhf.at[0], gwhr, gwhg,
+                                                             gwhf.at[1], gwh_send, gwh_recv)
+    gwo_start()
+
+    def gwo_out():
+        gwo_finish()
+        gwot_ref[0:GWO_HALF, :] = gwop[0]
+        gwot_ref[GWO_HALF:CLS, :] = gwop[1, 0:CLS - GWO_HALF, :]
+        loss_ref[...] = jnp.sum(gwop[1, GWO_HALF - 1:GWO_HALF, :], axis=1, keepdims=True) / label_count
+
+    reduce_pass(et, HID, D1_CHUNKS, part1, rb1, recv_b, d2d_b, {},
+                {0: [gwo_spread], 'mid': [gwo_collect], 'late': [gwo_out]})
+    gwhs[...] = dot_last(xall[0], con[0].astype(BF16))
+    gwh_start()
+    gwh_spread()
+    gwh_collect()
+    gwh_finish()
+    gwh_ref[0:GWH_HALF, :] = gwhp[0]
+    gwh_ref[GWH_HALF:F_IN, :] = gwhp[1, 0:F_IN - GWH_HALF, :]
 
 
 def device_step(adj_rows, feat_rows, w_hidden, w_output, labels, train_mask, block_mask):
-    mask_row = train_mask.astype(BF16)[None, :]
-    x_ext = jnp.concatenate([feat_rows.T, mask_row, jnp.zeros((F_PAD - F_IN - 1, BLK), BF16)], axis=0)
     dma = pltpu.SemaphoreType.DMA
     vmem = pl.BlockSpec(memory_space=pltpu.VMEM)
     hbm = pl.BlockSpec(memory_space=pl.ANY)
@@ -374,12 +427,13 @@
         name='gcn_step',
         out_shape=(jax.ShapeDtypeStruct((F_IN, HID), F32), jax.ShapeDtypeStruct((CLS, HID), F32),
                    jax.ShapeDtypeStruct((1, 1), F32)),
-        in_specs=[hbm, hbm, vmem, vmem, vmem, vmem, pl.BlockSpec(memory_space=pltpu.SMEM)],
+        in_specs=[hbm, vmem, vmem, vmem, vmem, vmem, pl.BlockSpec(memory_space=pltpu.SMEM)],
         out_specs=(vmem, vmem, vmem),
         scratch_shapes=[
             pltpu.VMEM((NB, BLK, BLK), BF16),
             pltpu.VMEM((NB, F_PAD, BLK), BF16),
             pltpu.VMEM((NB, CLS_PAD, BLK), BF16),
+            pltpu.VMEM((3, HID, BLK), BF16),
             pltpu.VMEM((BLK, HID), F32),
             pltpu.VMEM((HID, BLK), F32),
             pltpu.VMEM((BLK, CLS_PAD), F32),
@@ -395,19 +449,22 @@
             pltpu.VMEM((CLS_PAD, HID), BF16),
             pltpu.VMEM((16, BLK), F32),
             pltpu.VMEM((1, 128), F32),
+            pltpu.VMEM((CLS_PAD, HID), F32),
+            pltpu.VMEM((2, GWO_HALF, HID), F32),
+            pltpu.VMEM((GWO_HALF, HID), F32),
+            pltpu.VMEM((8, GWO_HALF, HID), F32),
+            pltpu.VMEM((2, GWO_HALF, HID), F32),
             pltpu.VMEM((F_PAD, HID), F32),
-            pltpu.VMEM((CLS_PAD, HID), F32),
-            pltpu.VMEM((2, AR_ROWS, HID), F32),
-            pltpu.VMEM((AR_ROWS, HID), F32),
-            pltpu.VMEM((AR_ROWS, HID), F32),
-            pltpu.VMEM((AR_ROWS, HID), F32),
-            pltpu.VMEM((8, AR_ROWS, HID), F32),
-            dma((NB,)), dma, dma((21,)), dma((8,)),
-            dma((21,)), dma((8,)), dma((21,)), dma((8,)), dma((21,)), dma((8,)), dma((21,)), dma((8,)),
-            dma((9,)), dma((9,)),
+            pltpu.VMEM((2, GWH_HALF, HID), F32),
+            pltpu.VMEM((GWH_HALF, HID), F32),
+            pltpu.VMEM((8, GWH_HALF, HID), F32),
+            pltpu.VMEM((2, GWH_HALF, HID), F32),
+            dma((NB,)), dma((21,)), dma((8,)),
+            dma((21,)), dma((8,)), dma((21,)), dma((8,)),
+            dma((9,)), dma((9,)), dma((9,)), dma((9,)),
         ],
         compiler_params=pltpu.CompilerParams(collective_id=0, has_side_effects=True, vmem_limit_bytes=67043328),
-    )(adj_rows, x_ext, w_hidden, w_output.T, labels[None, :], train_mask[None, :], block_mask)
+    )(adj_rows, feat_rows.T, w_hidden, w_output.T, labels[None, :], train_mask[None, :], block_mask)
     return loss[0, 0], gwh, gwot.T
 
 

time: 115 us -> 101 us (0.88)
  Pallas kernels: 107 us -> 95.2 us
  other arithmetic: 2.41 us -> 0 us
    pallas_call x1, Pallas kernels: 107 us -> 95.2 us  [device_step(): pl.pallas_call(step_kernel, name='gcn_step', out_shape=(jax.ShapeDtypeStr...]
    concatenate x1 -> x0, other arithmetic: 1.72 us -> none  [device_step(): jnp.concatenate([feat_rows.T, mask_row, jnp.zeros((F_PAD - F_IN - 1, BLK)...]
where the time goes in v2:
time: 101 us; the launch traced here: 100 us
  Pallas kernels  95.2 us (94%)
  local copies, waits for them, and re-layouts  2.78 us (3%)
  between operations  2.46 us (2%)
    pallas_call x1, Pallas kernels, device_step(): pl.pallas_call(step_kernel, name='gcn_step', out_shape=(jax.ShapeDtypeStr...  95.2 us
    unnamed x2, local copies, waits for them, and re-layouts  2.78 us

profile of v2, /device:TPU:0, one launch (start us, length us, event | category | flops | bytes accessed | tf_op | source)
XLA Modules:
  0.0 100.4 jit_solution(11283539147935942834)
XLA Ops:
  0.6 95.2 %gcn_step.1 = (f32[100,128]{1,0:T(8,128)}, f32[47,128]{1,0:T(8,128)}, f32[1,1]{1,0:T(1,128)}) custom-call(bf16[1024,16384]{1,0:T(8,128)(2,1)} %adj_hbm.1, bf16[100,1024]{1,0:T(8,128)(2,1)} %bitcast.6, f32[100,128]{1,0:T(8,128)} %wh_ref.1, f32[47,128]{1,0:T(8,128)} %bitcast.7, s32[1,1024]{1,0:T(1,128)} %bitcast.9, s32[1,1024]{1,0:T(1,128)} %bitcast.10, ...), custom_call_target="tpu_custom_call" | custom-call | tf_op jit(solution)/shard_map/gcn_step/pallas_call | solution.py:425
  96.5 1.4 %copy.14 = f32[100,128]{1,0:T(8,128)} copy(f32[100,128]{1,0:T(8,128)} %get-tuple-element.13) | data formatting | bytes 102400
  98.0 1.3 %copy.15 = f32[128,47]{0,1:T(8,128)} copy(f32[128,47]{0,1:T(8,128)} %bitcast.8) | data formatting | bytes 48128

commit v3 on v2

--- a/solution.py
+++ b/solution.py
@@ -20,7 +20,59 @@
 Y_CHUNKS = [(0, 16), (16, 16), (32, 16)]
 D1_CHUNKS = [(0, 48), (48, 40), (88, 40)]
 GWO_HALF, GWH_HALF = 24, 56
+OUT_ROWS = F_PAD + CLS_PAD
 M_TILE = 256
+
+
+def later_dims(q, k):
+    order = ORDERS[k]
+    return order[1 + max(order.index(d) for d in order if q & d):]
+
+
+def last_dim(q, k):
+    return max((d for d in ORDERS[k] if q & d), key=ORDERS[k].index)
+
+
+def plan_gather(sizes, cost, max_group):
+    link = {1: 0.0, 2: 0.0, 4: 0.0, 0: 0.0}
+    ops, arrive, relayed, ready = [], {}, {}, [0]
+    now = 0.0
+
+    def send(table, key, dim, size):
+        link[dim] = max(now, link[dim]) + size / (46.6 if dim else 600.0)
+        table[key] = link[dim] + (2.3 if dim else 0.95)
+
+    for j in range(3):
+        for k in range(3):
+            send(arrive, (ORDERS[k][j], k), ORDERS[k][j], sizes[k])
+    send(relayed, 0, 0, sum(sizes))
+    got = {q: 0 for q in range(8)}
+    while arrive or relayed or ready:
+        key = min(arrive, key=arrive.get, default=None)
+        if key is not None and arrive[key] <= now:
+            del arrive[key]
+            q, k = key
+            ops.append(('recv', q, k))
+            for d in later_dims(q, k):
+                send(arrive, (q | d, k), d, sizes[k])
+            got[q] += 1
+            if got[q] == 3:
+                ops.append(('relay', q))
+                send(relayed, q, 0, sum(sizes))
+                ready.append(2 * QI[q])
+            continue
+        for q in sorted(relayed, key=relayed.get):
+            if relayed[q] <= now:
+                del relayed[q]
+                ops.append(('take', q))
+                ready.append(2 * QI[q] + 1)
+        if ready:
+            ops.append(('dot', ready[:max_group]))
+            now += cost(len(ready[:max_group]))
+            ready = ready[max_group:]
+        else:
+            now = min(list(arrive.values()) + list(relayed.values()))
+    return ops
 
 
 def dot_last(lhs, rhs):
@@ -31,10 +83,11 @@
     return lax.dot_general(lhs, rhs, (((0,), (0,)), ((), ())), preferred_element_type=F32)
 
 
-def step_kernel(adj_hbm, x_ref, wh_ref, wot_ref, lab_ref, msk_ref, bm_ref, gwh_ref, gwot_ref, loss_ref,
+def step_kernel(adj_hbm, x_hbm, wh_hbm, wot_hbm, lab_hbm, msk_hbm, bm_hbm, out_ref,
+                x_ref, wh_ref, wot_ref, lab_ref, msk_ref, bm_ref,
                 adj, xall, yall, y1b, z1, z1t, z2, hid, gt, et, con, part2, part1, rb2, rb1, whs, wos, macc, lossv,
                 gwos, gwop, gwor, gwog, gwof, gwhs, gwhp, gwhr, gwhg, gwhf,
-                a_sem, ici_send, d2d_send, recv_a, d2d_a, recv_b, d2d_b,
+                io_sem, a_sem, ici_send, d2d_send, recv_a, d2d_a, recv_b, d2d_b,
                 gwo_send, gwo_recv, gwh_send, gwh_recv):
     me = lax.axis_index(AXIS_NAME)
     coords = [me % 2, (me // 2) % 2, (me // 4) % 2, me // 8]
@@ -55,27 +108,34 @@
     def a_copy(slot, blk=0):
         return pltpu.make_async_copy(adj_hbm.at[:, pl.ds(pl.multiple_of(blk * BLK, BLK), BLK)], adj.at[slot], a_sem.at[slot])
 
-    a_order = [0, 1, 2, 4, 6, 3, 5, 7, 8, 10, 12, 9, 11, 13, 14, 15]
+    plan1 = plan_gather([n * 2.048 for _, n in X_CHUNKS], lambda n: 0.2 + 0.54 * n, 2)
+    a_order = [slot for op in plan1 if op[0] == 'dot' for slot in op[1]]
 
     def start_a(lo, hi):
         for slot in a_order[lo:hi]:
             a_copy(slot, dev(rel_of(slot))).start()
 
-    start_a(0, 6)
+    loads = [pltpu.make_async_copy(src, dst, io_sem.at[n]) for n, (src, dst) in enumerate(
+        [(x_hbm, x_ref), (wh_hbm, wh_ref), (wot_hbm, wot_ref), (lab_hbm, lab_ref), (msk_hbm, msk_ref), (bm_hbm, bm_ref)])]
     barrier = pltpu.get_barrier_semaphore()
     peers = [1] + [2 * q for q in range(1, 8)]
     for rel in peers:
         pl.semaphore_signal(barrier, inc=1, device_id=(dev(rel),), device_id_type=MESH)
 
-    xall[0, 0:F_PAD - 8, :] = x_ref[0:F_PAD - 8, :]
-    xall[0, F_PAD - 8:F_PAD, :] = jnp.concatenate([x_ref[F_PAD - 8:F_IN, :], jnp.zeros((F_PAD - F_IN, BLK), BF16)], axis=0)
-    whs[...] = jnp.zeros_like(whs)
-    whs[0:F_IN, :] = wh_ref[...].astype(BF16)
-    wos[...] = jnp.zeros_like(wos)
-    wos[0:CLS, :] = wot_ref[...].astype(BF16)
+    for load in loads:
+        load.start()
+    start_a(0, 6)
     macc[...] = jnp.zeros_like(macc)
     z1[...] = jnp.zeros_like(z1)
     z2[...] = jnp.zeros_like(z2)
+    whs[...] = jnp.zeros_like(whs)
+    wos[...] = jnp.zeros_like(wos)
+    for load in loads:
+        load.wait()
+    xall[0, 0:F_PAD - 8, :] = x_ref[0:F_PAD - 8, :]
+    xall[0, F_PAD - 8:F_PAD, :] = jnp.concatenate([x_ref[F_PAD - 8:F_IN, :], jnp.zeros((F_PAD - F_IN, BLK), BF16)], axis=0)
+    whs[0:F_IN, :] = wh_ref[...].astype(BF16)
+    wos[0:CLS, :] = wot_ref[...].astype(BF16)
     pl.semaphore_wait(barrier, len(peers))
 
     def mask_of(slot):
@@ -97,114 +157,36 @@
         return bm_ref[me, total]
 
 
-    def ag_ops(buf, chunks, recv, recv_d2d):
+    def gather_product(buf, chunks, recv, recv_d2d, ops, first, dots):
         def ici(src_q, dim, k):
             dst_q = src_q ^ dim
             lo, n = chunks[k]
-            idx = k * 7 + QI[dst_q] - 1
             return rcopy(buf.at[2 * QI[src_q], pl.ds(lo, n), :], buf.at[2 * QI[dst_q], pl.ds(lo, n), :],
-                         ici_send.at[idx], recv.at[idx], 2 * dim)
-
-        def d2d(q_idx):
-            return rcopy(buf.at[2 * q_idx], buf.at[2 * q_idx + 1], d2d_send.at[q_idx], recv_d2d.at[q_idx], 1)
-
-        def recv_wait(dst_q, k):
-            o = ORDERS[k]
-            dim = max((d for d in o if dst_q & d), key=o.index)
-            ici(dst_q ^ dim, dim, k).wait_recv()
-
-        def send_own():
-            for j in range(3):
-                for k in range(3):
-                    ici(0, ORDERS[k][j], k).start()
-            d2d(0).start()
-
-        def near():
+                         ici_send, recv.at[k * 7 + QI[dst_q] - 1], 2 * dim)
+
+        def relay(q):
+            return rcopy(buf.at[2 * QI[q]], buf.at[2 * QI[q] + 1], d2d_send, recv_d2d.at[QI[q]], 1)
+
+        for j in range(3):
             for k in range(3):
-                a, b, c = ORDERS[k]
-                recv_wait(a, k)
-                ici(a, b, k).start()
-                ici(a, c, k).start()
-            for k in range(3):
-                a, b, c = ORDERS[k]
-                recv_wait(b, k)
-                ici(b, c, k).start()
-
-        def near_last():
-            for k in range(3):
-                recv_wait(ORDERS[k][2], k)
-            for q in (1, 2, 4):
-                d2d(QI[q]).start()
-
-        def mid():
-            for k in range(3):
-                a, b, c = ORDERS[k]
-                recv_wait(a | b, k)
-                ici(a | b, c, k).start()
-
-        def mid_last():
-            for k in range(3):
-                recv_wait(ORDERS[k][0] | ORDERS[k][2], k)
-            for k in range(3):
-                recv_wait(ORDERS[k][1] | ORDERS[k][2], k)
-            for q in (3, 5, 6):
-                d2d(QI[q]).start()
-
-        def far():
-            for k in range(3):
-                recv_wait(7, k)
-            d2d(QI[7]).start()
-
-        def wait_sends():
-            for k in range(3):
-                o = ORDERS[k]
-                for q in range(1, 8):
-                    dim = max((d for d in o if q & d), key=o.index)
-                    ici(q ^ dim, dim, k).wait_send()
-            for i in range(8):
-                d2d(i).wait_send()
-
-        return dict(d2d=d2d, send_own=send_own, near=near, near_last=near_last, mid=mid, mid_last=mid_last, far=far,
-                    wait_sends=wait_sends)
-
-    def forward_pass(ag, compute):
-        compute([0])
-        ag['near']()
-        ag['d2d'](0).wait_recv()
-        compute([1])
-        ag['near_last']()
-
-        def group(g, carry):
-            base = 2 + (g % 2) + 6 * (g // 2)
-
-            @pl.when(g == 1)
-            def _():
-                ag['mid']()
-                for q in (1, 2, 4):
-                    ag['d2d'](QI[q]).wait_recv()
-
-            @pl.when(g == 2)
-            def _():
-                ag['mid_last']()
-
-            @pl.when(g == 3)
-            def _():
-                ag['far']()
-                for q in (3, 5, 6):
-                    ag['d2d'](QI[q]).wait_recv()
-
-            compute([base, base + 2, base + 4])
-            return carry
-
-        lax.fori_loop(0, 4, group, 0)
-        compute([14])
-        ag['d2d'](7).wait_recv()
-        compute([15])
-        ag['wait_sends']()
-
-    ag1 = ag_ops(xall, X_CHUNKS, recv_a, d2d_a)
-    ag1['send_own']()
-    start_a(6, 16)
+                ici(0, ORDERS[k][j], k).start()
+        relay(0).start()
+        first()
+        for op, q, *k in ops:
+            if op == 'dot':
+                dots(q)
+            elif op == 'take':
+                relay(q).wait_recv()
+            elif op == 'relay':
+                relay(q).start()
+            else:
+                d = last_dim(q, k[0])
+                ici(q ^ d, d, k[0]).wait_recv()
+                for d in later_dims(q, k[0]):
+                    ici(q, d, k[0]).start()
+        for count, sem, rel in ((7, ici_send, 2), (8, d2d_send, 1)):
+            sent = buf.at[pl.ds(0, count)]
+            rcopy(sent, sent, sem, recv.at[0], rel).wait_send()
 
     def accumulate(out, slots, blocks):
         for lo in range(0, BLK, M_TILE):
@@ -213,7 +195,7 @@
                 acc = acc + dot_last(adj[slot, lo:lo + M_TILE, :], block)
             out[lo:lo + M_TILE, :] = acc
 
-    def compute1(slots):
+    def dots1(slots):
         for slot in slots:
             a_copy(slot).wait()
         for j, slot in enumerate(slots):
@@ -221,24 +203,25 @@
             y1b[j] = (yt.astype(F32) * mask_of(slot).astype(F32)).astype(BF16)
         accumulate(z1, slots, [y1b[j] for j in range(len(slots))])
 
-    forward_pass(ag1, compute1)
-
-    hid[...] = jnp.maximum(z1[...], 0.0).astype(BF16)
+    gather_product(xall, X_CHUNKS, recv_a, d2d_a, plan1, lambda: start_a(6, 16), dots1)
+
     cls_id = lax.broadcasted_iota(jnp.int32, (CLS_PAD, BLK), 0)
     weight = msk_ref[...].astype(F32)
+    hid[...] = jnp.maximum(z1[...], 0.0).astype(BF16)
     yall[0] = jnp.where(cls_id == CLS, weight, dot_last(wos[...], hid[...])).astype(BF16)
-    ag2 = ag_ops(yall, Y_CHUNKS, recv_b, d2d_b)
-    ag2['send_own']()
-    z1t[...] = jnp.transpose(z1[...])
-
-    def compute2(slots):
+
+    def dots2(slots):
         blocks = []
         for slot in slots:
             macc[...] += yall[slot, CLS_PAD - 16:CLS_PAD, :].astype(F32)
             blocks.append((yall[slot].astype(F32) * mask_of(slot).astype(F32)).astype(BF16))
         accumulate(z2, slots, blocks)
 
-    forward_pass(ag2, compute2)
+    def keep_sign():
+        z1t[...] = jnp.transpose(z1[...])
+
+    plan2 = plan_gather([n * 2.048 for _, n in Y_CHUNKS], lambda n: 0.13 + 0.54 * n, 2)
+    gather_product(yall, Y_CHUNKS, recv_b, d2d_b, plan2, keep_sign, dots2)
     label_count = jnp.sum(macc[15:16, :])
 
     zt = jnp.transpose(z2[...])
@@ -265,11 +248,11 @@
         def ici(q, k):
             lo, n = chunks[k]
             idx = k * 7 + QI[q] - 1
-            return rcopy(con.at[2 * QI[q], pl.ds(lo, n), :], rb.at[QI[q] - 1, pl.ds(lo, n), :], ici_send.at[idx],
+            return rcopy(con.at[2 * QI[q], pl.ds(lo, n), :], rb.at[QI[q] - 1, pl.ds(lo, n), :], ici_send,
                          recv.at[idx], 2 * dim_of(q, k))
 
         def d2d(i):
-            return rcopy(con.at[2 * i + 1, pl.ds(0, rows), :], part.at[i], d2d_send.at[i], recv_d2d.at[i], 1)
+            return rcopy(con.at[2 * i + 1, pl.ds(0, rows), :], part.at[i], d2d_send, recv_d2d.at[i], 1)
 
         def sources(q, k):
             out = []
@@ -345,11 +328,9 @@
         for hook in hooks.get('late', ()):
             hook()
         take_rank(0, 2)
-        for k in range(3):
-            for q in range(1, 8):
-                ici(q, k).wait_send()
-        for i in range(8):
-            d2d(i).wait_send()
+        for count, sem, rel in ((7, ici_send, 2), (8, d2d_send, 1)):
+            sent = con.at[pl.ds(0, count), pl.ds(0, rows), :]
+            rcopy(sent, sent, sem, recv.at[0], rel).wait_send()
 
     reduce_pass(gt, CLS_PAD, Y_CHUNKS, part2, rb2, recv_a, d2d_a, {6: [0], 7: [1]}, {})
     d2t = con[0, 0:CLS_PAD, :].astype(BF16)
@@ -368,8 +349,8 @@
                 halves[1, total_rows - rows:rows, :] = jnp.zeros((2 * rows - total_rows, HID), F32)
 
         pair = rcopy(halves.at[1 - core], other, send.at[0], recv.at[0], 1)
-        sends = [rcopy(gathered.at[0], gathered.at[q], send.at[q], recv.at[q], 2 * q) for q in range(1, 8)]
-        back = rcopy(own, final, send.at[8], recv.at[8], 1)
+        sends = [rcopy(gathered.at[0], gathered.at[q], send.at[1], recv.at[q], 2 * q) for q in range(1, 8)]
+        back = rcopy(own, final, send.at[2], recv.at[8], 1)
 
         def start():
             prepare()
@@ -383,7 +364,8 @@
 
         def collect():
             for cp in sends:
-                cp.wait()
+                cp.wait_recv()
+            rcopy(gathered.at[pl.ds(0, 7)], gathered.at[pl.ds(0, 7)], send.at[1], recv.at[0], 2).wait_send()
             g = gathered
             own[...] = ((g[0] + g[1]) + (g[2] + g[3])) + ((g[4] + g[5]) + (g[6] + g[7]))
             back.start()
@@ -403,9 +385,10 @@
 
     def gwo_out():
         gwo_finish()
-        gwot_ref[0:GWO_HALF, :] = gwop[0]
-        gwot_ref[GWO_HALF:CLS, :] = gwop[1, 0:CLS - GWO_HALF, :]
-        loss_ref[...] = jnp.sum(gwop[1, GWO_HALF - 1:GWO_HALF, :], axis=1, keepdims=True) / label_count
+        out_ref[F_PAD:F_PAD + GWO_HALF, :] = gwop[0]
+        out_ref[F_PAD + GWO_HALF:OUT_ROWS, :] = gwop[1]
+        loss = jnp.sum(gwop[1, GWO_HALF - 1:GWO_HALF, :], axis=1, keepdims=True) / label_count
+        out_ref[OUT_ROWS - 1:OUT_ROWS, :] = jnp.broadcast_to(loss, (1, HID))
 
     reduce_pass(et, HID, D1_CHUNKS, part1, rb1, recv_b, d2d_b, {},
                 {0: [gwo_spread], 'mid': [gwo_collect], 'late': [gwo_out]})
@@ -414,26 +397,37 @@
     gwh_spread()
     gwh_collect()
     gwh_finish()
-    gwh_ref[0:GWH_HALF, :] = gwhp[0]
-    gwh_ref[GWH_HALF:F_IN, :] = gwhp[1, 0:F_IN - GWH_HALF, :]
+    out_ref[0:GWH_HALF, :] = gwhp[0]
+    out_ref[GWH_HALF:F_PAD, :] = gwhp[1, 0:F_PAD - GWH_HALF, :]
+
+
+def split_kernel(sums_ref, gwh_ref, gwot_ref, loss_ref):
+    gwh_ref[...] = sums_ref[0:F_IN, :]
+    gwot_ref[...] = sums_ref[F_PAD:F_PAD + CLS, :]
+    loss_ref[...] = sums_ref[OUT_ROWS - 1:OUT_ROWS, 0:1]
 
 
 def device_step(adj_rows, feat_rows, w_hidden, w_output, labels, train_mask, block_mask):
     dma = pltpu.SemaphoreType.DMA
     vmem = pl.BlockSpec(memory_space=pltpu.VMEM)
     hbm = pl.BlockSpec(memory_space=pl.ANY)
-    gwh, gwot, loss = pl.pallas_call(
+    sums = pl.pallas_call(
         step_kernel,
         name='gcn_step',
-        out_shape=(jax.ShapeDtypeStruct((F_IN, HID), F32), jax.ShapeDtypeStruct((CLS, HID), F32),
-                   jax.ShapeDtypeStruct((1, 1), F32)),
-        in_specs=[hbm, vmem, vmem, vmem, vmem, vmem, pl.BlockSpec(memory_space=pltpu.SMEM)],
-        out_specs=(vmem, vmem, vmem),
+        out_shape=jax.ShapeDtypeStruct((OUT_ROWS, HID), F32),
+        in_specs=[hbm] * 7,
+        out_specs=vmem,
         scratch_shapes=[
+            pltpu.VMEM((F_IN, BLK), BF16),
+            pltpu.VMEM((F_IN, HID), F32),
+            pltpu.VMEM((CLS, HID), F32),
+            pltpu.VMEM((1, BLK), jnp.int32),
+            pltpu.VMEM((1, BLK), jnp.int32),
+            pltpu.SMEM((NB, NB), jnp.int32),
             pltpu.VMEM((NB, BLK, BLK), BF16),
             pltpu.VMEM((NB, F_PAD, BLK), BF16),
             pltpu.VMEM((NB, CLS_PAD, BLK), BF16),
-            pltpu.VMEM((3, HID, BLK), BF16),
+            pltpu.VMEM((2, HID, BLK), BF16),
             pltpu.VMEM((BLK, HID), F32),
             pltpu.VMEM((HID, BLK), F32),
             pltpu.VMEM((BLK, CLS_PAD), F32),
@@ -459,12 +453,19 @@
             pltpu.VMEM((GWH_HALF, HID), F32),
             pltpu.VMEM((8, GWH_HALF, HID), F32),
             pltpu.VMEM((2, GWH_HALF, HID), F32),
-            dma((NB,)), dma((21,)), dma((8,)),
-            dma((21,)), dma((8,)), dma((21,)), dma((8,)),
-            dma((9,)), dma((9,)), dma((9,)), dma((9,)),
+            dma((6,)), dma((NB,)), dma, dma, dma((21,)), dma((8,)), dma((21,)), dma((8,)),
+            dma((3,)), dma((9,)), dma((3,)), dma((9,)),
         ],
         compiler_params=pltpu.CompilerParams(collective_id=0, has_side_effects=True, vmem_limit_bytes=67043328),
     )(adj_rows, feat_rows.T, w_hidden, w_output.T, labels[None, :], train_mask[None, :], block_mask)
+    gwh, gwot, loss = pl.pallas_call(
+        split_kernel,
+        name='split_sums',
+        out_shape=(jax.ShapeDtypeStruct((F_IN, HID), F32), jax.ShapeDtypeStruct((CLS, HID), F32),
+                   jax.ShapeDtypeStruct((1, 1), F32)),
+        in_specs=[vmem],
+        out_specs=(vmem, vmem, vmem),
+    )(sums)
     return loss[0, 0], gwh, gwot.T
 
 

time: 101 us -> 97.4 us (0.964)
  local copies, waits for them, and re-layouts: 2.78 us -> 0 us
  between operations: 2.46 us -> 0.64 us
  Pallas kernels: 95.2 us -> 96.6 us
    unnamed x2 -> x0, local copies, waits for them, and re-layouts: 2.78 us -> none
    pallas_call x1 -> x2, Pallas kernels: 95.2 us -> 96.6 us  [the longest x1 95.1 us: device_step(): pl.pallas_call(step_kernel, name='gcn_step', out_shape=jax.ShapeDtypeStru...]
where the time goes in v3:
time: 97.4 us; the launch traced here: 97.3 us
  Pallas kernels  96.6 us (99%)
    pallas_call x1, Pallas kernels, device_step(): pl.pallas_call(step_kernel, name='gcn_step', out_shape=jax.ShapeDtypeStru...  95.1 us

profile of v3, /device:TPU:0, one launch (start us, length us, event | category | flops | bytes accessed | tf_op | source)
XLA Modules:
  0.0 97.3 jit_solution(10884650160144386059)
XLA Ops:
  0.6 95.1 %gcn_step.1.sums_ref = f32[152,128]{1,0:T(8,128)} custom-call(bf16[1024,16384]{1,0:T(8,128)(2,1)} %adj_hbm.1, bf16[100,1024]{1,0:T(8,128)(2,1)} %bitcast.6, f32[100,128]{1,0:T(8,128)} %wh_hbm.1, f32[47,128]{1,0:T(8,128)} %bitcast.7, s32[1,1024]{1,0:T(1,128)} %bitcast.8, s32[1,1024]{1,0:T(1,128)} %bitcast.9, s32[16,16]{1,0:T(8,128)} %bm_hbm.1), custom_call_target="tpu_custom_call" | custom-call | tf_op jit(solution)/shard_map/gcn_step/pallas_call | solution.py:414
  95.7 1.5 %split_sums.1 = (f32[100,128]{1,0:T(8,128)}, f32[47,128]{1,0:T(8,128)}, f32[1,1]{1,0:T(1,128)}) custom-call(f32[152,128]{1,0:T(8,128)} %gcn_step.1.sums_ref), custom_call_target="tpu_custom_call" | custom-call | tf_op jit(solution)/shard_map/split_sums/pallas_call | solution.py:461

commit v4 on v3

--- a/solution.py
+++ b/solution.py
@@ -18,10 +18,13 @@
 ORDERS = [(1, 2, 4), (2, 4, 1), (4, 1, 2)]
 X_CHUNKS = [(0, 40), (40, 32), (72, 32)]
 Y_CHUNKS = [(0, 16), (16, 16), (32, 16)]
-D1_CHUNKS = [(0, 48), (48, 40), (88, 40)]
+D2_CHUNKS = [(lo, n, 0, BLK, k) for k, (lo, n) in enumerate(Y_CHUNKS)]
+D1_CHUNKS = [(0, 40, 0, BLK, 0), (40, 40, 0, BLK, 1), (80, 40, 0, BLK, 2),
+             (120, 8, 0, 384, 0), (120, 8, 384, 384, 1), (120, 8, 768, 256, 2)]
 GWO_HALF, GWH_HALF = 24, 56
 OUT_ROWS = F_PAD + CLS_PAD
 M_TILE = 256
+A_AHEAD = 5
 
 
 def later_dims(q, k):
@@ -118,13 +121,13 @@
     loads = [pltpu.make_async_copy(src, dst, io_sem.at[n]) for n, (src, dst) in enumerate(
         [(x_hbm, x_ref), (wh_hbm, wh_ref), (wot_hbm, wot_ref), (lab_hbm, lab_ref), (msk_hbm, msk_ref), (bm_hbm, bm_ref)])]
     barrier = pltpu.get_barrier_semaphore()
-    peers = [1] + [2 * q for q in range(1, 8)]
+    peers = [1, 2, 4, 8]
     for rel in peers:
         pl.semaphore_signal(barrier, inc=1, device_id=(dev(rel),), device_id_type=MESH)
 
     for load in loads:
         load.start()
-    start_a(0, 6)
+    start_a(0, A_AHEAD)
     macc[...] = jnp.zeros_like(macc)
     z1[...] = jnp.zeros_like(z1)
     z2[...] = jnp.zeros_like(z2)
@@ -198,12 +201,14 @@
     def dots1(slots):
         for slot in slots:
             a_copy(slot).wait()
+            ahead = a_order.index(slot) + A_AHEAD
+            start_a(ahead, ahead + 1)
         for j, slot in enumerate(slots):
             yt = dot_first(whs[...], xall[slot]).astype(BF16)
             y1b[j] = (yt.astype(F32) * mask_of(slot).astype(F32)).astype(BF16)
         accumulate(z1, slots, [y1b[j] for j in range(len(slots))])
 
-    gather_product(xall, X_CHUNKS, recv_a, d2d_a, plan1, lambda: start_a(6, 16), dots1)
+    gather_product(xall, X_CHUNKS, recv_a, d2d_a, plan1, lambda: None, dots1)
 
     cls_id = lax.broadcasted_iota(jnp.int32, (CLS_PAD, BLK), 0)
     weight = msk_ref[...].astype(F32)
@@ -242,13 +247,19 @@
 
 
     def reduce_pass(lhs_ref, rows, chunks, part, rb, recv, recv_d2d, early, hooks):
+        parts = range(len(chunks))
+
+        def order_of(k):
+            return ORDERS[chunks[k][4]]
+
         def dim_of(q, k):
-            return next(d for d in reversed(ORDERS[k]) if q & d)
+            return next(d for d in reversed(order_of(k)) if q & d)
 
         def ici(q, k):
-            lo, n = chunks[k]
+            lo, n, lane, lanes, _ = chunks[k]
             idx = k * 7 + QI[q] - 1
-            return rcopy(con.at[2 * QI[q], pl.ds(lo, n), :], rb.at[QI[q] - 1, pl.ds(lo, n), :], ici_send,
+            return rcopy(con.at[2 * QI[q], pl.ds(lo, n), pl.ds(lane, lanes)],
+                         rb.at[QI[q] - 1, pl.ds(lo, n), pl.ds(lane, lanes)], ici_send,
                          recv.at[idx], 2 * dim_of(q, k))
 
         def d2d(i):
@@ -256,7 +267,7 @@
 
         def sources(q, k):
             out = []
-            for d in reversed(ORDERS[k]):
+            for d in reversed(order_of(k)):
                 if q & d:
                     break
                 out.append(q ^ d)
@@ -266,22 +277,22 @@
             lhs = (lhs_ref[...].astype(F32) * mask_of(slot).astype(F32)).astype(BF16)
             con[slot, 0:rows, :] = jnp.dot(lhs, adj[slot], preferred_element_type=F32)
 
-        waiting = {(q, k): set(sources(q, k)) for q in range(8) for k in range(3)}
+        waiting = {(q, k): set(sources(q, k)) for q in range(8) for k in parts}
 
         def pair_sum(q):
             i = QI[q]
             d2d(i).wait_recv()
             con[2 * i, 0:rows, :] += part[i]
-            for k in range(3):
+            for k in parts:
                 if q and not waiting[q, k]:
                     ici(q, k).start()
 
         def take(src, k):
             d = dim_of(src, k)
             q = src ^ d
-            lo, n = chunks[k]
+            lo, n, lane, lanes, _ = chunks[k]
             ici(src, k).wait_recv()
-            con[2 * QI[q], lo:lo + n, :] += rb[QI[src] - 1, lo:lo + n, :]
+            con[2 * QI[q], lo:lo + n, lane:lane + lanes] += rb[QI[src] - 1, lo:lo + n, lane:lane + lanes]
             waiting[q, k].discard(src)
             if q and not waiting[q, k]:
                 ici(q, k).start()
@@ -306,12 +317,12 @@
         taken = set()
 
         def sources_of(k, phase):
-            d = ORDERS[k][2 - phase]
-            later = [e for e in ORDERS[k][3 - phase:]]
+            d = order_of(k)[2 - phase]
+            later = order_of(k)[3 - phase:]
             return sorted((q for q in range(1, 8) if q & d and not any(q & e for e in later)), key=rank.get)
 
         def take_rank(r, phase=0):
-            for k in range(3):
+            for k in parts:
                 take(sources_of(k, phase)[r], k)
                 taken.add((phase, r))
 
@@ -332,7 +343,7 @@
             sent = con.at[pl.ds(0, count), pl.ds(0, rows), :]
             rcopy(sent, sent, sem, recv.at[0], rel).wait_send()
 
-    reduce_pass(gt, CLS_PAD, Y_CHUNKS, part2, rb2, recv_a, d2d_a, {6: [0], 7: [1]}, {})
+    reduce_pass(gt, CLS_PAD, D2_CHUNKS, part2, rb2, recv_a, d2d_a, {6: [0], 7: [1]}, {})
     d2t = con[0, 0:CLS_PAD, :].astype(BF16)
     gwo = jnp.dot(d2t, hid[...], preferred_element_type=F32)
     et[...] = jnp.where(z1t[...] > 0, dot_first(wos[...], d2t), 0.0).astype(BF16)
@@ -453,7 +464,7 @@
             pltpu.VMEM((GWH_HALF, HID), F32),
             pltpu.VMEM((8, GWH_HALF, HID), F32),
             pltpu.VMEM((2, GWH_HALF, HID), F32),
-            dma((6,)), dma((NB,)), dma, dma, dma((21,)), dma((8,)), dma((21,)), dma((8,)),
+            dma((6,)), dma((NB,)), dma, dma, dma((21,)), dma((8,)), dma((42,)), dma((8,)),
             dma((3,)), dma((9,)), dma((3,)), dma((9,)),
         ],
         compiler_params=pltpu.CompilerParams(collective_id=0, has_side_effects=True, vmem_limit_bytes=67043328),

time: 97.4 us -> 95.3 us (0.978)
  Pallas kernels: 96.6 us -> 94.5 us
    pallas_call x1, Pallas kernels: 95.1 us -> 93 us  [device_step(): pl.pallas_call(step_kernel, name='gcn_step', out_shape=jax.ShapeDtypeStru...]
where the time goes in v4:
time: 95.3 us; the launch traced here: 95.2 us
  Pallas kernels  94.5 us (99%)
    pallas_call x1, Pallas kernels, device_step(): pl.pallas_call(step_kernel, name='gcn_step', out_shape=jax.ShapeDtypeStru...  93 us

profile of v4, /device:TPU:0, one launch (start us, length us, event | category | flops | bytes accessed | tf_op | source)
XLA Modules:
  0.0 95.2 jit_solution(17147843365060169703)
XLA Ops:
  0.6 93.0 %gcn_step.1.sums_ref = f32[152,128]{1,0:T(8,128)} custom-call(bf16[1024,16384]{1,0:T(8,128)(2,1)} %adj_hbm.1, bf16[100,1024]{1,0:T(8,128)(2,1)} %bitcast.6, f32[100,128]{1,0:T(8,128)} %wh_hbm.1, f32[47,128]{1,0:T(8,128)} %bitcast.7, s32[1,1024]{1,0:T(1,128)} %bitcast.8, s32[1,1024]{1,0:T(1,128)} %bitcast.9, s32[16,16]{1,0:T(8,128)} %bm_hbm.1), custom_call_target="tpu_custom_call" | custom-call | tf_op jit(solution)/shard_map/gcn_step/pallas_call | solution.py:425
  93.6 1.5 %split_sums.1 = (f32[100,128]{1,0:T(8,128)}, f32[47,128]{1,0:T(8,128)}, f32[1,1]{1,0:T(1,128)}) custom-call(f32[152,128]{1,0:T(8,128)} %gcn_step.1.sums_ref), custom_call_target="tpu_custom_call" | custom-call | tf_op jit(solution)/shard_map/split_sums/pallas_call | solution.py:472

commit v5 on v4

--- a/solution.py
+++ b/solution.py
@@ -27,9 +27,14 @@
 A_AHEAD = 5
 
 
-def later_dims(q, k):
+def forwards(q, k):
+    first, second, third = ORDERS[k]
+    if k == 2 and q == first:
+        return [(first, second)]
+    if k == 2 and q == second:
+        return [(second, third), (first, third)]
     order = ORDERS[k]
-    return order[1 + max(order.index(d) for d in order if q & d):]
+    return [(q, d) for d in order[1 + max(order.index(d) for d in order if q & d):]]
 
 
 def last_dim(q, k):
@@ -56,8 +61,8 @@
             del arrive[key]
             q, k = key
             ops.append(('recv', q, k))
-            for d in later_dims(q, k):
-                send(arrive, (q | d, k), d, sizes[k])
+            for src, d in forwards(q, k):
+                send(arrive, (src | d, k), d, sizes[k])
             got[q] += 1
             if got[q] == 3:
                 ops.append(('relay', q))
@@ -185,8 +190,8 @@
             else:
                 d = last_dim(q, k[0])
                 ici(q ^ d, d, k[0]).wait_recv()
-                for d in later_dims(q, k[0]):
-                    ici(q, d, k[0]).start()
+                for src, d in forwards(q, k[0]):
+                    ici(src, d, k[0]).start()
         for count, sem, rel in ((7, ici_send, 2), (8, d2d_send, 1)):
             sent = buf.at[pl.ds(0, count)]
             rcopy(sent, sent, sem, recv.at[0], rel).wait_send()
@@ -425,7 +430,7 @@
     sums = pl.pallas_call(
         step_kernel,
         name='gcn_step',
-        out_shape=jax.ShapeDtypeStruct((OUT_ROWS, HID), F32),
+        out_shape=pltpu.VMEM((OUT_ROWS, HID), F32),
         in_specs=[hbm] * 7,
         out_specs=vmem,
         scratch_shapes=[
@@ -467,7 +472,7 @@
             dma((6,)), dma((NB,)), dma, dma, dma((21,)), dma((8,)), dma((42,)), dma((8,)),
             dma((3,)), dma((9,)), dma((3,)), dma((9,)),
         ],
-        compiler_params=pltpu.CompilerParams(collective_id=0, has_side_effects=True, vmem_limit_bytes=67043328),
+        compiler_params=pltpu.CompilerParams(collective_id=0, has_side_effects=True, vmem_limit_bytes=62000000),
     )(adj_rows, feat_rows.T, w_hidden, w_output.T, labels[None, :], train_mask[None, :], block_mask)
     gwh, gwot, loss = pl.pallas_call(
         split_kernel,
@@ -476,7 +481,7 @@
                    jax.ShapeDtypeStruct((1, 1), F32)),
         in_specs=[vmem],
         out_specs=(vmem, vmem, vmem),
-    )(sums)
+    )(pltpu.with_memory_space_constraint(sums, pltpu.VMEM))
     return loss[0, 0], gwh, gwot.T
 
 

time: 95.3 us -> 93.2 us (0.978)
  Pallas kernels: 94.5 us -> 92.4 us
    pallas_call x1, Pallas kernels: 93 us -> 91.7 us  [device_step(): pl.pallas_call(step_kernel, name='gcn_step', out_shape=pltpu.VMEM((OUT_RO...]
where the time goes in v5:
time: 93.2 us; the launch traced here: 93 us
  Pallas kernels  92.4 us (99%)
    pallas_call x1, Pallas kernels, device_step(): pl.pallas_call(step_kernel, name='gcn_step', out_shape=pltpu.VMEM((OUT_RO...  91.7 us

profile of v5, /device:TPU:0, one launch (start us, length us, event | category | flops | bytes accessed | tf_op | source)
XLA Modules:
  0.0 93.0 jit_solution(6986357247037378017)
XLA Ops:
  0.6 91.7 %gcn_step.1.sums_ref = f32[152,128]{1,0:T(8,128)S(1)} custom-call(bf16[1024,16384]{1,0:T(8,128)(2,1)} %adj_hbm.1, bf16[100,1024]{1,0:T(8,128)(2,1)} %bitcast.6, f32[100,128]{1,0:T(8,128)} %wh_hbm.1, f32[47,128]{1,0:T(8,128)} %bitcast.7, s32[1,1024]{1,0:T(1,128)} %bitcast.8, s32[1,1024]{1,0:T(1,128)} %bitcast.9, s32[16,16]{1,0:T(8,128)} %bm_hbm.1), custom_call_target="tpu_custom_call" | custom-call | tf_op jit(solution)/shard_map/gcn_step/pallas_call | solution.py:430
  92.4 0.6 split_sums.1

commit v6 on v5

--- a/solution.py
+++ b/solution.py
@@ -13,7 +13,7 @@
 F_IN, F_PAD = 100, 104
 HID = 128
 CLS, CLS_PAD = 47, 48
-QS = [0, 1, 2, 4, 3, 5, 6, 7]
+QS = [0, 2, 4, 1, 3, 6, 5, 7]
 QI = {q: i for i, q in enumerate(QS)}
 ORDERS = [(1, 2, 4), (2, 4, 1), (4, 1, 2)]
 X_CHUNKS = [(0, 40), (40, 32), (72, 32)]
@@ -27,11 +27,11 @@
 A_AHEAD = 5
 
 
-def forwards(q, k):
+def forwards(q, k, swapped):
     first, second, third = ORDERS[k]
-    if k == 2 and q == first:
+    if k in swapped and q == first:
         return [(first, second)]
-    if k == 2 and q == second:
+    if k in swapped and q == second:
         return [(second, third), (first, third)]
     order = ORDERS[k]
     return [(q, d) for d in order[1 + max(order.index(d) for d in order if q & d):]]
@@ -41,7 +41,7 @@
     return max((d for d in ORDERS[k] if q & d), key=ORDERS[k].index)
 
 
-def plan_gather(sizes, cost, max_group):
+def plan_gather(sizes, cost, max_group, swapped):
     link = {1: 0.0, 2: 0.0, 4: 0.0, 0: 0.0}
     ops, arrive, relayed, ready = [], {}, {}, [0]
     now = 0.0
@@ -61,7 +61,7 @@
             del arrive[key]
             q, k = key
             ops.append(('recv', q, k))
-            for src, d in forwards(q, k):
+            for src, d in forwards(q, k, swapped):
                 send(arrive, (src | d, k), d, sizes[k])
             got[q] += 1
             if got[q] == 3:
@@ -93,7 +93,7 @@
 
 def step_kernel(adj_hbm, x_hbm, wh_hbm, wot_hbm, lab_hbm, msk_hbm, bm_hbm, out_ref,
                 x_ref, wh_ref, wot_ref, lab_ref, msk_ref, bm_ref,
-                adj, xall, yall, y1b, z1, z1t, z2, hid, gt, et, con, part2, part1, rb2, rb1, whs, wos, macc, lossv,
+                adj, xall, yall, y1b, z1, z1t, z2, z2t, turned, hid, gt, et, con, part2, part1, rb2, rb1, whs, wos, macc, lossv,
                 gwos, gwop, gwor, gwog, gwof, gwhs, gwhp, gwhr, gwhg, gwhf,
                 io_sem, a_sem, ici_send, d2d_send, recv_a, d2d_a, recv_b, d2d_b,
                 gwo_send, gwo_recv, gwh_send, gwh_recv):
@@ -116,7 +116,7 @@
     def a_copy(slot, blk=0):
         return pltpu.make_async_copy(adj_hbm.at[:, pl.ds(pl.multiple_of(blk * BLK, BLK), BLK)], adj.at[slot], a_sem.at[slot])
 
-    plan1 = plan_gather([n * 2.048 for _, n in X_CHUNKS], lambda n: 0.2 + 0.54 * n, 2)
+    plan1 = plan_gather([n * 2.048 for _, n in X_CHUNKS], lambda n: 0.2 + 0.54 * n, 2, (2,))
     a_order = [slot for op in plan1 if op[0] == 'dot' for slot in op[1]]
 
     def start_a(lo, hi):
@@ -136,6 +136,7 @@
     macc[...] = jnp.zeros_like(macc)
     z1[...] = jnp.zeros_like(z1)
     z2[...] = jnp.zeros_like(z2)
+    z2t[...] = jnp.zeros_like(z2t)
     whs[...] = jnp.zeros_like(whs)
     wos[...] = jnp.zeros_like(wos)
     for load in loads:
@@ -165,7 +166,7 @@
         return bm_ref[me, total]
 
 
-    def gather_product(buf, chunks, recv, recv_d2d, ops, first, dots):
+    def gather_product(buf, chunks, recv, recv_d2d, ops, swapped, first, dots):
         def ici(src_q, dim, k):
             dst_q = src_q ^ dim
             lo, n = chunks[k]
@@ -190,7 +191,7 @@
             else:
                 d = last_dim(q, k[0])
                 ici(q ^ d, d, k[0]).wait_recv()
-                for src, d in forwards(q, k[0]):
+                for src, d in forwards(q, k[0], swapped):
                     ici(src, d, k[0]).start()
         for count, sem, rel in ((7, ici_send, 2), (8, d2d_send, 1)):
             sent = buf.at[pl.ds(0, count)]
@@ -213,7 +214,7 @@
             y1b[j] = (yt.astype(F32) * mask_of(slot).astype(F32)).astype(BF16)
         accumulate(z1, slots, [y1b[j] for j in range(len(slots))])
 
-    gather_product(xall, X_CHUNKS, recv_a, d2d_a, plan1, lambda: None, dots1)
+    gather_product(xall, X_CHUNKS, recv_a, d2d_a, plan1, (2,), lambda: None, dots1)
 
     cls_id = lax.broadcasted_iota(jnp.int32, (CLS_PAD, BLK), 0)
     weight = msk_ref[...].astype(F32)
@@ -225,16 +226,26 @@
         for slot in slots:
             macc[...] += yall[slot, CLS_PAD - 16:CLS_PAD, :].astype(F32)
             blocks.append((yall[slot].astype(F32) * mask_of(slot).astype(F32)).astype(BF16))
-        accumulate(z2, slots, blocks)
+        if len(slots) == 1:
+            accumulate(z2, slots, blocks)
+            return
+        stream, held = slots
+        turned[0] = jnp.transpose(adj[held, 0:M_TILE, :])
+        for n in range(BLK // M_TILE):
+            tile = slice(M_TILE * n, M_TILE * (n + 1))
+            if n + 1 < BLK // M_TILE:
+                turned[(n + 1) % 2] = jnp.transpose(adj[held, M_TILE * (n + 1):M_TILE * (n + 2), :])
+            z2[tile, :] += dot_last(adj[stream, tile, :], blocks[0])
+            z2t[:, tile] += jnp.dot(blocks[1], turned[n % 2], preferred_element_type=F32)
 
     def keep_sign():
         z1t[...] = jnp.transpose(z1[...])
 
-    plan2 = plan_gather([n * 2.048 for _, n in Y_CHUNKS], lambda n: 0.13 + 0.54 * n, 2)
-    gather_product(yall, Y_CHUNKS, recv_b, d2d_b, plan2, keep_sign, dots2)
+    plan2 = plan_gather([n * 2.048 for _, n in Y_CHUNKS], lambda n: 0.43 + 0.25 * n, 2, (0, 1))
+    gather_product(yall, Y_CHUNKS, recv_b, d2d_b, plan2, (0, 1), keep_sign, dots2)
     label_count = jnp.sum(macc[15:16, :])
 
-    zt = jnp.transpose(z2[...])
+    zt = jnp.transpose(z2[...]) + z2t[...]
     valid = cls_id < CLS
     top = jnp.max(jnp.where(valid, zt, -jnp.inf), axis=0, keepdims=True)
     expz = jnp.where(valid, jnp.exp(zt - top), 0.0)
@@ -251,7 +262,7 @@
     gt[...] = jnp.where(valid, grad, 0.0).astype(BF16)
 
 
-    def reduce_pass(lhs_ref, rows, chunks, part, rb, recv, recv_d2d, early, hooks):
+    def reduce_pass(lhs_ref, rows, chunks, part, rb, recv, recv_d2d, early, tail, hooks):
         parts = range(len(chunks))
 
         def order_of(k):
@@ -319,7 +330,6 @@
             return carry
 
         rank = {q: r for r, q in enumerate(reversed(QS))}
-        taken = set()
 
         def sources_of(k, phase):
             d = order_of(k)[2 - phase]
@@ -329,26 +339,21 @@
         def take_rank(r, phase=0):
             for k in parts:
                 take(sources_of(k, phase)[r], k)
-                taken.add((phase, r))
 
         lax.fori_loop(0, 8, body, 0)
-        for r in range(4):
-            if (0, r) not in taken:
-                take_rank(r)
-            if r == 2:
-                for hook in hooks.get('mid', ()):
+        for step in tail:
+            if step is None:
+                pair_sum(0)
+            elif isinstance(step, str):
+                for hook in hooks[step]:
                     hook()
-                pair_sum(0)
-        take_rank(0, 1)
-        take_rank(1, 1)
-        for hook in hooks.get('late', ()):
-            hook()
-        take_rank(0, 2)
+            else:
+                take_rank(step[1], step[0])
         for count, sem, rel in ((7, ici_send, 2), (8, d2d_send, 1)):
             sent = con.at[pl.ds(0, count), pl.ds(0, rows), :]
             rcopy(sent, sent, sem, recv.at[0], rel).wait_send()
 
-    reduce_pass(gt, CLS_PAD, D2_CHUNKS, part2, rb2, recv_a, d2d_a, {6: [0], 7: [1]}, {})
+    reduce_pass(gt, CLS_PAD, D2_CHUNKS, part2, rb2, recv_a, d2d_a, {5: [0], 6: [1], 7: [2]}, [None, (1, 0), (0, 3), (1, 1), (2, 0)], {})
     d2t = con[0, 0:CLS_PAD, :].astype(BF16)
     gwo = jnp.dot(d2t, hid[...], preferred_element_type=F32)
     et[...] = jnp.where(z1t[...] > 0, dot_first(wos[...], d2t), 0.0).astype(BF16)
@@ -407,6 +412,7 @@
         out_ref[OUT_ROWS - 1:OUT_ROWS, :] = jnp.broadcast_to(loss, (1, HID))
 
     reduce_pass(et, HID, D1_CHUNKS, part1, rb1, recv_b, d2d_b, {},
+                [(0, 0), (0, 1), (0, 2), 'mid', None, (0, 3), (1, 0), (1, 1), 'late', (2, 0)],
                 {0: [gwo_spread], 'mid': [gwo_collect], 'late': [gwo_out]})
     gwhs[...] = dot_last(xall[0], con[0].astype(BF16))
     gwh_start()
@@ -447,6 +453,8 @@
             pltpu.VMEM((BLK, HID), F32),
             pltpu.VMEM((HID, BLK), F32),
             pltpu.VMEM((BLK, CLS_PAD), F32),
+            pltpu.VMEM((CLS_PAD, BLK), F32),
+            pltpu.VMEM((2, BLK, M_TILE), BF16),
             pltpu.VMEM((BLK, HID), BF16),
             pltpu.VMEM((CLS_PAD, BLK), BF16),
             pltpu.VMEM((HID, BLK), BF16),
@@ -472,7 +480,7 @@
             dma((6,)), dma((NB,)), dma, dma, dma((21,)), dma((8,)), dma((42,)), dma((8,)),
             dma((3,)), dma((9,)), dma((3,)), dma((9,)),
         ],
-        compiler_params=pltpu.CompilerParams(collective_id=0, has_side_effects=True, vmem_limit_bytes=62000000),
+        compiler_params=pltpu.CompilerParams(collective_id=0, has_side_effects=True, vmem_limit_bytes=64000000),
     )(adj_rows, feat_rows.T, w_hidden, w_output.T, labels[None, :], train_mask[None, :], block_mask)
     gwh, gwot, loss = pl.pallas_call(
         split_kernel,

time: 93.2 us -> 91.4 us (0.981)
  Pallas kernels: 92.4 us -> 90.6 us
    pallas_call x1, Pallas kernels: 91.7 us -> 90 us  [device_step(): pl.pallas_call(step_kernel, name='gcn_step', out_shape=pltpu.VMEM((OUT_RO...]
where the time goes in v6:
time: 91.4 us; the launch traced here: 91.3 us
  Pallas kernels  90.6 us (99%)
    pallas_call x1, Pallas kernels, device_step(): pl.pallas_call(step_kernel, name='gcn_step', out_shape=pltpu.VMEM((OUT_RO...  90 us

profile of v6, /device:TPU:0, one launch (start us, length us, event | category | flops | bytes accessed | tf_op | source)
XLA Modules:
  0.0 91.3 jit_solution(17000612725060203734)
XLA Ops:
  0.6 90.0 %gcn_step.1.sums_ref = f32[152,128]{1,0:T(8,128)S(1)} custom-call(bf16[1024,16384]{1,0:T(8,128)(2,1)} %adj_hbm.1, bf16[100,1024]{1,0:T(8,128)(2,1)} %bitcast.6, f32[100,128]{1,0:T(8,128)} %wh_hbm.1, f32[47,128]{1,0:T(8,128)} %bitcast.7, s32[1,1024]{1,0:T(1,128)} %bitcast.8, s32[1,1024]{1,0:T(1,128)} %bitcast.9, s32[16,16]{1,0:T(8,128)} %bm_hbm.1), custom_call_target="tpu_custom_call" | custom-call | tf_op jit(solution)/shard_map/gcn_step/pallas_call | solution.py:436
  90.6 0.6 split_sums.1

commit v7 on v6

--- a/solution.py
+++ b/solution.py
@@ -16,9 +16,9 @@
 QS = [0, 2, 4, 1, 3, 6, 5, 7]
 QI = {q: i for i, q in enumerate(QS)}
 ORDERS = [(1, 2, 4), (2, 4, 1), (4, 1, 2)]
-X_CHUNKS = [(0, 40), (40, 32), (72, 32)]
-Y_CHUNKS = [(0, 16), (16, 16), (32, 16)]
-D2_CHUNKS = [(lo, n, 0, BLK, k) for k, (lo, n) in enumerate(Y_CHUNKS)]
+X_CHUNKS = [(0, 32, 0, BLK, 0), (32, 32, 0, BLK, 1), (64, 32, 0, BLK, 2),
+            (96, 8, 0, 384, 0), (96, 8, 384, 384, 1), (96, 8, 768, 256, 2)]
+Y_CHUNKS = [(0, 16, 0, BLK, 0), (16, 16, 0, BLK, 1), (32, 16, 0, BLK, 2)]
 D1_CHUNKS = [(0, 40, 0, BLK, 0), (40, 40, 0, BLK, 1), (80, 40, 0, BLK, 2),
              (120, 8, 0, 384, 0), (120, 8, 384, 384, 1), (120, 8, 768, 256, 2)]
 GWO_HALF, GWH_HALF = 24, 56
@@ -27,21 +27,21 @@
 A_AHEAD = 5
 
 
-def forwards(q, k, swapped):
-    first, second, third = ORDERS[k]
-    if k in swapped and q == first:
+def forwards(q, order_id, swapped):
+    first, second, third = order = ORDERS[order_id]
+    if order_id in swapped and q == first:
         return [(first, second)]
-    if k in swapped and q == second:
+    if order_id in swapped and q == second:
         return [(second, third), (first, third)]
-    order = ORDERS[k]
     return [(q, d) for d in order[1 + max(order.index(d) for d in order if q & d):]]
 
 
-def last_dim(q, k):
-    return max((d for d in ORDERS[k] if q & d), key=ORDERS[k].index)
-
-
-def plan_gather(sizes, cost, max_group, swapped):
+def last_dim(q, order_id):
+    return max((d for d in ORDERS[order_id] if q & d), key=ORDERS[order_id].index)
+
+
+def plan_gather(chunks, cost, max_group, swapped):
+    sizes = [n * lanes * 0.002 for _, n, _, lanes, _ in chunks]
     link = {1: 0.0, 2: 0.0, 4: 0.0, 0: 0.0}
     ops, arrive, relayed, ready = [], {}, {}, [0]
     now = 0.0
@@ -51,8 +51,9 @@
         table[key] = link[dim] + (2.3 if dim else 0.95)
 
     for j in range(3):
-        for k in range(3):
-            send(arrive, (ORDERS[k][j], k), ORDERS[k][j], sizes[k])
+        for k, chunk in enumerate(chunks):
+            d = ORDERS[chunk[4]][j]
+            send(arrive, (d, k), d, sizes[k])
     send(relayed, 0, 0, sum(sizes))
     got = {q: 0 for q in range(8)}
     while arrive or relayed or ready:
@@ -61,10 +62,10 @@
             del arrive[key]
             q, k = key
             ops.append(('recv', q, k))
-            for src, d in forwards(q, k, swapped):
+            for src, d in forwards(q, chunks[k][4], swapped):
                 send(arrive, (src | d, k), d, sizes[k])
             got[q] += 1
-            if got[q] == 3:
+            if got[q] == len(chunks):
                 ops.append(('relay', q))
                 send(relayed, q, 0, sum(sizes))
                 ready.append(2 * QI[q])
@@ -116,7 +117,7 @@
     def a_copy(slot, blk=0):
         return pltpu.make_async_copy(adj_hbm.at[:, pl.ds(pl.multiple_of(blk * BLK, BLK), BLK)], adj.at[slot], a_sem.at[slot])
 
-    plan1 = plan_gather([n * 2.048 for _, n in X_CHUNKS], lambda n: 0.2 + 0.54 * n, 2, (2,))
+    plan1 = plan_gather(X_CHUNKS, lambda n: 0.2 + 0.54 * n, 2, (2,))
     a_order = [slot for op in plan1 if op[0] == 'dot' for slot in op[1]]
 
     def start_a(lo, hi):
@@ -169,16 +170,17 @@
     def gather_product(buf, chunks, recv, recv_d2d, ops, swapped, first, dots):
         def ici(src_q, dim, k):
             dst_q = src_q ^ dim
-            lo, n = chunks[k]
-            return rcopy(buf.at[2 * QI[src_q], pl.ds(lo, n), :], buf.at[2 * QI[dst_q], pl.ds(lo, n), :],
+            lo, n, lane, lanes, _ = chunks[k]
+            return rcopy(buf.at[2 * QI[src_q], pl.ds(lo, n), pl.ds(lane, lanes)],
+                         buf.at[2 * QI[dst_q], pl.ds(lo, n), pl.ds(lane, lanes)],
                          ici_send, recv.at[k * 7 + QI[dst_q] - 1], 2 * dim)
 
         def relay(q):
             return rcopy(buf.at[2 * QI[q]], buf.at[2 * QI[q] + 1], d2d_send, recv_d2d.at[QI[q]], 1)
 
         for j in range(3):
-            for k in range(3):
-                ici(0, ORDERS[k][j], k).start()
+            for k, chunk in enumerate(chunks):
+                ici(0, ORDERS[chunk[4]][j], k).start()
         relay(0).start()
         first()
         for op, q, *k in ops:
@@ -189,9 +191,10 @@
             elif op == 'relay':
                 relay(q).start()
             else:
-                d = last_dim(q, k[0])
+                order_id = chunks[k[0]][4]
+                d = last_dim(q, order_id)
                 ici(q ^ d, d, k[0]).wait_recv()
-                for src, d in forwards(q, k[0], swapped):
+                for src, d in forwards(q, order_id, swapped):
                     ici(src, d, k[0]).start()
         for count, sem, rel in ((7, ici_send, 2), (8, d2d_send, 1)):
             sent = buf.at[pl.ds(0, count)]
@@ -241,7 +244,7 @@
     def keep_sign():
         z1t[...] = jnp.transpose(z1[...])
 
-    plan2 = plan_gather([n * 2.048 for _, n in Y_CHUNKS], lambda n: 0.43 + 0.25 * n, 2, (0, 1))
+    plan2 = plan_gather(Y_CHUNKS, lambda n: 0.43 + 0.25 * n, 2, (0, 1))
     gather_product(yall, Y_CHUNKS, recv_b, d2d_b, plan2, (0, 1), keep_sign, dots2)
     label_count = jnp.sum(macc[15:16, :])
 
@@ -281,6 +284,12 @@
         def d2d(i):
             return rcopy(con.at[2 * i + 1, pl.ds(0, rows), :], part.at[i], d2d_send, recv_d2d.at[i], 1)
 
+        cuts = [chunks[0][0], chunks[1][0], chunks[2][0], rows]
+
+        def d2d_part(p):
+            span = pl.ds(cuts[p], cuts[p + 1] - cuts[p])
+            return rcopy(con.at[15, span, :], part.at[7, span, :], d2d_send, recv_d2d.at[8 + p if p else 7], 1)
+
         def sources(q, k):
             out = []
             for d in reversed(order_of(k)):
@@ -297,11 +306,13 @@
 
         def pair_sum(q):
             i = QI[q]
-            d2d(i).wait_recv()
-            con[2 * i, 0:rows, :] += part[i]
-            for k in parts:
-                if q and not waiting[q, k]:
-                    ici(q, k).start()
+            for p in range(3) if i == 7 else [None]:
+                lo, hi = (0, rows) if p is None else (cuts[p], cuts[p + 1])
+                (d2d(i) if p is None else d2d_part(p)).wait_recv()
+                con[2 * i, lo:hi, :] += part[i, lo:hi, :]
+                for k in parts:
+                    if q and not waiting[q, k] and lo <= chunks[k][0] < hi:
+                        ici(q, k).start()
 
         def take(src, k):
             d = dim_of(src, k)
@@ -316,7 +327,16 @@
         def body(n, carry):
             i = 7 - n
             compute(2 * i + 1)
-            d2d(i).start()
+
+            @pl.when(n == 0)
+            def _():
+                for p in range(3):
+                    d2d_part(p).start()
+
+            @pl.when(n > 0)
+            def _():
+                d2d(i).start()
+
             compute(2 * i)
             for m in range(8):
                 @pl.when(n == m)
@@ -353,7 +373,7 @@
             sent = con.at[pl.ds(0, count), pl.ds(0, rows), :]
             rcopy(sent, sent, sem, recv.at[0], rel).wait_send()
 
-    reduce_pass(gt, CLS_PAD, D2_CHUNKS, part2, rb2, recv_a, d2d_a, {5: [0], 6: [1], 7: [2]}, [None, (1, 0), (0, 3), (1, 1), (2, 0)], {})
+    reduce_pass(gt, CLS_PAD, Y_CHUNKS, part2, rb2, recv_a, d2d_a, {5: [0], 6: [1], 7: [2]}, [None, (1, 0), (0, 3), (1, 1), (2, 0)], {})
     d2t = con[0, 0:CLS_PAD, :].astype(BF16)
     gwo = jnp.dot(d2t, hid[...], preferred_element_type=F32)
     et[...] = jnp.where(z1t[...] > 0, dot_first(wos[...], d2t), 0.0).astype(BF16)
@@ -477,7 +497,7 @@
             pltpu.VMEM((GWH_HALF, HID), F32),
             pltpu.VMEM((8, GWH_HALF, HID), F32),
             pltpu.VMEM((2, GWH_HALF, HID), F32),
-            dma((6,)), dma((NB,)), dma, dma, dma((21,)), dma((8,)), dma((42,)), dma((8,)),
+            dma((6,)), dma((NB,)), dma, dma, dma((42,)), dma((11,)), dma((42,)), dma((11,)),
             dma((3,)), dma((9,)), dma((3,)), dma((9,)),
         ],
         compiler_params=pltpu.CompilerParams(collective_id=0, has_side_effects=True, vmem_limit_bytes=64000000),

time: 91.4 us -> 91.6 us (level)
  no operation moved by 1% of the time
where the time goes in v7:
time: 91.6 us; the launch traced here: 91.5 us
  Pallas kernels  90.9 us (99%)
    pallas_call x1, Pallas kernels, device_step(): pl.pallas_call(step_kernel, name='gcn_step', out_shape=pltpu.VMEM((OUT_RO...  90.2 us

profile of v7, /device:TPU:0, one launch (start us, length us, event | category | flops | bytes accessed | tf_op | source)
XLA Modules:
  0.0 91.5 jit_solution(9688739097117657546)
XLA Ops:
  0.6 90.2 %gcn_step.1.sums_ref = f32[152,128]{1,0:T(8,128)S(1)} custom-call(bf16[1024,16384]{1,0:T(8,128)(2,1)} %adj_hbm.1, bf16[100,1024]{1,0:T(8,128)(2,1)} %bitcast.6, f32[100,128]{1,0:T(8,128)} %wh_hbm.1, f32[47,128]{1,0:T(8,128)} %bitcast.7, s32[1,1024]{1,0:T(1,128)} %bitcast.8, s32[1,1024]{1,0:T(1,128)} %bitcast.9, s32[16,16]{1,0:T(8,128)} %bm_hbm.1), custom_call_target="tpu_custom_call" | custom-call | tf_op jit(solution)/shard_map/gcn_step/pallas_call | solution.py:456
  90.9 0.6 split_sums.1

commit v8 on v7

--- a/solution.py
+++ b/solution.py
@@ -16,8 +16,7 @@
 QS = [0, 2, 4, 1, 3, 6, 5, 7]
 QI = {q: i for i, q in enumerate(QS)}
 ORDERS = [(1, 2, 4), (2, 4, 1), (4, 1, 2)]
-X_CHUNKS = [(0, 32, 0, BLK, 0), (32, 32, 0, BLK, 1), (64, 32, 0, BLK, 2),
-            (96, 8, 0, 384, 0), (96, 8, 384, 384, 1), (96, 8, 768, 256, 2)]
+X_CHUNKS = [(0, 40, 0, BLK, 0), (40, 32, 0, BLK, 1), (72, 32, 0, BLK, 2)]
 Y_CHUNKS = [(0, 16, 0, BLK, 0), (16, 16, 0, BLK, 1), (32, 16, 0, BLK, 2)]
 D1_CHUNKS = [(0, 40, 0, BLK, 0), (40, 40, 0, BLK, 1), (80, 40, 0, BLK, 2),
              (120, 8, 0, 384, 0), (120, 8, 384, 384, 1), (120, 8, 768, 256, 2)]
@@ -497,7 +496,7 @@
             pltpu.VMEM((GWH_HALF, HID), F32),
             pltpu.VMEM((8, GWH_HALF, HID), F32),
             pltpu.VMEM((2, GWH_HALF, HID), F32),
-            dma((6,)), dma((NB,)), dma, dma, dma((42,)), dma((11,)), dma((42,)), dma((11,)),
+            dma((6,)), dma((NB,)), dma, dma, dma((21,)), dma((11,)), dma((42,)), dma((11,)),
             dma((3,)), dma((9,)), dma((3,)), dma((9,)),
         ],
         compiler_params=pltpu.CompilerParams(collective_id=0, has_side_effects=True, vmem_limit_bytes=64000000),

time: 91.6 us -> 91.3 us (level)
  no operation moved by 1% of the time
where the time goes in v8:
time: 91.3 us; the launch traced here: 91.2 us
  Pallas kernels  90.5 us (99%)
    pallas_call x1, Pallas kernels, device_step(): pl.pallas_call(step_kernel, name='gcn_step', out_shape=pltpu.VMEM((OUT_RO...  89.9 us

profile of v8, /device:TPU:0, one launch (start us, length us, event | category | flops | bytes accessed | tf_op | source)
XLA Modules:
  0.0 91.2 jit_solution(5606967646083992871)
XLA Ops:
  0.6 89.9 %gcn_step.1.sums_ref = f32[152,128]{1,0:T(8,128)S(1)} custom-call(bf16[1024,16384]{1,0:T(8,128)(2,1)} %adj_hbm.1, bf16[100,1024]{1,0:T(8,128)(2,1)} %bitcast.6, f32[100,128]{1,0:T(8,128)} %wh_hbm.1, f32[47,128]{1,0:T(8,128)} %bitcast.7, s32[1,1024]{1,0:T(1,128)} %bitcast.8, s32[1,1024]{1,0:T(1,128)} %bitcast.9, s32[16,16]{1,0:T(8,128)} %bm_hbm.1), custom_call_target="tpu_custom_call" | custom-call | tf_op jit(solution)/shard_map/gcn_step/pallas_call | solution.py:455
  90.5 0.6 split_sums.1

commit v9 on v8

--- a/solution.py
+++ b/solution.py
@@ -93,7 +93,7 @@
 
 def step_kernel(adj_hbm, x_hbm, wh_hbm, wot_hbm, lab_hbm, msk_hbm, bm_hbm, out_ref,
                 x_ref, wh_ref, wot_ref, lab_ref, msk_ref, bm_ref,
-                adj, xall, yall, y1b, z1, z1t, z2, z2t, turned, hid, gt, et, con, part2, part1, rb2, rb1, whs, wos, macc, lossv,
+                adj, xall, yall, y1b, z1, z1t, z2, z2t, turned, hidt, gt, et, con, part2, part1, rb2, rb1, whs, wos, macc, lossv,
                 gwos, gwop, gwor, gwog, gwof, gwhs, gwhp, gwhr, gwhg, gwhf,
                 io_sem, a_sem, ici_send, d2d_send, recv_a, d2d_a, recv_b, d2d_b,
                 gwo_send, gwo_recv, gwh_send, gwh_recv):
@@ -116,7 +116,7 @@
     def a_copy(slot, blk=0):
         return pltpu.make_async_copy(adj_hbm.at[:, pl.ds(pl.multiple_of(blk * BLK, BLK), BLK)], adj.at[slot], a_sem.at[slot])
 
-    plan1 = plan_gather(X_CHUNKS, lambda n: 0.2 + 0.54 * n, 2, (2,))
+    plan1 = plan_gather(X_CHUNKS, lambda n: 0.42 + 0.32 * n, 2, (2,))
     a_order = [slot for op in plan1 if op[0] == 'dot' for slot in op[1]]
 
     def start_a(lo, hi):
@@ -135,6 +135,7 @@
     start_a(0, A_AHEAD)
     macc[...] = jnp.zeros_like(macc)
     z1[...] = jnp.zeros_like(z1)
+    z1t[...] = jnp.zeros_like(z1t)
     z2[...] = jnp.zeros_like(z2)
     z2t[...] = jnp.zeros_like(z2t)
     whs[...] = jnp.zeros_like(whs)
@@ -199,12 +200,19 @@
             sent = buf.at[pl.ds(0, count)]
             rcopy(sent, sent, sem, recv.at[0], rel).wait_send()
 
-    def accumulate(out, slots, blocks):
-        for lo in range(0, BLK, M_TILE):
-            acc = out[lo:lo + M_TILE, :]
-            for slot, block in zip(slots, blocks):
-                acc = acc + dot_last(adj[slot, lo:lo + M_TILE, :], block)
-            out[lo:lo + M_TILE, :] = acc
+    def products(out, out_t, slots, blocks):
+        if len(slots) == 1:
+            for lo in range(0, BLK, M_TILE):
+                out[lo:lo + M_TILE, :] += dot_last(adj[slots[0], lo:lo + M_TILE, :], blocks[0])
+            return
+        stream, held = slots
+        turned[0] = jnp.transpose(adj[held, 0:M_TILE, :])
+        for n in range(BLK // M_TILE):
+            tile = slice(M_TILE * n, M_TILE * (n + 1))
+            if n + 1 < BLK // M_TILE:
+                turned[(n + 1) % 2] = jnp.transpose(adj[held, M_TILE * (n + 1):M_TILE * (n + 2), :])
+            out[tile, :] += dot_last(adj[stream, tile, :], blocks[0])
+            out_t[:, tile] += jnp.dot(blocks[1], turned[n % 2], preferred_element_type=F32)
 
     def dots1(slots):
         for slot in slots:
@@ -214,37 +222,25 @@
         for j, slot in enumerate(slots):
             yt = dot_first(whs[...], xall[slot]).astype(BF16)
             y1b[j] = (yt.astype(F32) * mask_of(slot).astype(F32)).astype(BF16)
-        accumulate(z1, slots, [y1b[j] for j in range(len(slots))])
+        products(z1, z1t, slots, [y1b[j] for j in range(len(slots))])
 
     gather_product(xall, X_CHUNKS, recv_a, d2d_a, plan1, (2,), lambda: None, dots1)
 
     cls_id = lax.broadcasted_iota(jnp.int32, (CLS_PAD, BLK), 0)
     weight = msk_ref[...].astype(F32)
-    hid[...] = jnp.maximum(z1[...], 0.0).astype(BF16)
-    yall[0] = jnp.where(cls_id == CLS, weight, dot_last(wos[...], hid[...])).astype(BF16)
+    z1t[...] += jnp.transpose(z1[...])
+    hidt[...] = jnp.maximum(z1t[...], 0.0).astype(BF16)
+    yall[0] = jnp.where(cls_id == CLS, weight, jnp.dot(wos[...], hidt[...], preferred_element_type=F32)).astype(BF16)
 
     def dots2(slots):
         blocks = []
         for slot in slots:
             macc[...] += yall[slot, CLS_PAD - 16:CLS_PAD, :].astype(F32)
             blocks.append((yall[slot].astype(F32) * mask_of(slot).astype(F32)).astype(BF16))
-        if len(slots) == 1:
-            accumulate(z2, slots, blocks)
-            return
-        stream, held = slots
-        turned[0] = jnp.transpose(adj[held, 0:M_TILE, :])
-        for n in range(BLK // M_TILE):
-            tile = slice(M_TILE * n, M_TILE * (n + 1))
-            if n + 1 < BLK // M_TILE:
-                turned[(n + 1) % 2] = jnp.transpose(adj[held, M_TILE * (n + 1):M_TILE * (n + 2), :])
-            z2[tile, :] += dot_last(adj[stream, tile, :], blocks[0])
-            z2t[:, tile] += jnp.dot(blocks[1], turned[n % 2], preferred_element_type=F32)
-
-    def keep_sign():
-        z1t[...] = jnp.transpose(z1[...])
+        products(z2, z2t, slots, blocks)
 
     plan2 = plan_gather(Y_CHUNKS, lambda n: 0.43 + 0.25 * n, 2, (0, 1))
-    gather_product(yall, Y_CHUNKS, recv_b, d2d_b, plan2, (0, 1), keep_sign, dots2)
+    gather_product(yall, Y_CHUNKS, recv_b, d2d_b, plan2, (0, 1), lambda: None, dots2)
     label_count = jnp.sum(macc[15:16, :])
 
     zt = jnp.transpose(z2[...]) + z2t[...]
@@ -374,8 +370,7 @@
 
     reduce_pass(gt, CLS_PAD, Y_CHUNKS, part2, rb2, recv_a, d2d_a, {5: [0], 6: [1], 7: [2]}, [None, (1, 0), (0, 3), (1, 1), (2, 0)], {})
     d2t = con[0, 0:CLS_PAD, :].astype(BF16)
-    gwo = jnp.dot(d2t, hid[...], preferred_element_type=F32)
-    et[...] = jnp.where(z1t[...] > 0, dot_first(wos[...], d2t), 0.0).astype(BF16)
+    gwo = dot_last(d2t, hidt[...])
     row_id = lax.broadcasted_iota(jnp.int32, (CLS_PAD, HID), 0)
     gwos[...] = jnp.where(row_id == CLS, lossv[...], gwo)
 
@@ -422,6 +417,7 @@
     gwh_start, gwh_spread, gwh_collect, gwh_finish = all_sum(GWH_HALF, F_PAD, gwhs, gwhp, gwhf.at[0], gwhr, gwhg,
                                                              gwhf.at[1], gwh_send, gwh_recv)
     gwo_start()
+    et[...] = jnp.where(z1t[...] > 0, dot_first(wos[...], d2t), 0.0).astype(BF16)
 
     def gwo_out():
         gwo_finish()
@@ -474,7 +470,7 @@
             pltpu.VMEM((BLK, CLS_PAD), F32),
             pltpu.VMEM((CLS_PAD, BLK), F32),
             pltpu.VMEM((2, BLK, M_TILE), BF16),
-            pltpu.VMEM((BLK, HID), BF16),
+            pltpu.VMEM((HID, BLK), BF16),
             pltpu.VMEM((CLS_PAD, BLK), BF16),
             pltpu.VMEM((HID, BLK), BF16),
             pltpu.VMEM((NB, HID, BLK), F32),

time: 91.3 us -> 91.4 us (level)
  no operation moved by 1% of the time
where the time goes in v9:
time: 91.4 us; the launch traced here: 91.3 us
  Pallas kernels  90.6 us (99%)
    pallas_call x1, Pallas kernels, device_step(): pl.pallas_call(step_kernel, name='gcn_step', out_shape=pltpu.VMEM((OUT_RO...  90 us

profile of v9, /device:TPU:0, one launch (start us, length us, event | category | flops | bytes accessed | tf_op | source)
XLA Modules:
  0.0 91.3 jit_solution(17134636656546218375)
XLA Ops:
  0.6 90.0 %gcn_step.1.sums_ref = f32[152,128]{1,0:T(8,128)S(1)} custom-call(bf16[1024,16384]{1,0:T(8,128)(2,1)} %adj_hbm.1, bf16[100,1024]{1,0:T(8,128)(2,1)} %bitcast.6, f32[100,128]{1,0:T(8,128)} %wh_hbm.1, f32[47,128]{1,0:T(8,128)} %bitcast.7, s32[1,1024]{1,0:T(1,128)} %bitcast.8, s32[1,1024]{1,0:T(1,128)} %bitcast.9, s32[16,16]{1,0:T(8,128)} %bm_hbm.1), custom_call_target="tpu_custom_call" | custom-call | tf_op jit(solution)/shard_map/gcn_step/pallas_call | solution.py:451
  90.6 0.6 split_sums.1

commit v10 on v8

--- a/solution.py
+++ b/solution.py
@@ -18,6 +18,7 @@
 ORDERS = [(1, 2, 4), (2, 4, 1), (4, 1, 2)]
 X_CHUNKS = [(0, 40, 0, BLK, 0), (40, 32, 0, BLK, 1), (72, 32, 0, BLK, 2)]
 Y_CHUNKS = [(0, 16, 0, BLK, 0), (16, 16, 0, BLK, 1), (32, 16, 0, BLK, 2)]
+D2_CHUNKS = [(8 * n, 8, 0, BLK, n % 3) for n in range(6)]
 D1_CHUNKS = [(0, 40, 0, BLK, 0), (40, 40, 0, BLK, 1), (80, 40, 0, BLK, 2),
              (120, 8, 0, 384, 0), (120, 8, 384, 384, 1), (120, 8, 768, 256, 2)]
 GWO_HALF, GWH_HALF = 24, 56
@@ -283,7 +284,7 @@
         def d2d(i):
             return rcopy(con.at[2 * i + 1, pl.ds(0, rows), :], part.at[i], d2d_send, recv_d2d.at[i], 1)
 
-        cuts = [chunks[0][0], chunks[1][0], chunks[2][0], rows]
+        cuts = [0, rows // 24 * 8, rows // 24 * 16, rows]
 
         def d2d_part(p):
             span = pl.ds(cuts[p], cuts[p + 1] - cuts[p])
@@ -372,7 +373,8 @@
             sent = con.at[pl.ds(0, count), pl.ds(0, rows), :]
             rcopy(sent, sent, sem, recv.at[0], rel).wait_send()
 
-    reduce_pass(gt, CLS_PAD, Y_CHUNKS, part2, rb2, recv_a, d2d_a, {5: [0], 6: [1], 7: [2]}, [None, (1, 0), (0, 3), (1, 1), (2, 0)], {})
+    reduce_pass(gt, CLS_PAD, D2_CHUNKS, part2, rb2, recv_a, d2d_a, {6: [0], 7: [1]},
+                [None, (0, 2), (1, 0), (0, 3), (1, 1), (2, 0)], {})
     d2t = con[0, 0:CLS_PAD, :].astype(BF16)
     gwo = jnp.dot(d2t, hid[...], preferred_element_type=F32)
     et[...] = jnp.where(z1t[...] > 0, dot_first(wos[...], d2t), 0.0).astype(BF16)
@@ -496,7 +498,7 @@
             pltpu.VMEM((GWH_HALF, HID), F32),
             pltpu.VMEM((8, GWH_HALF, HID), F32),
             pltpu.VMEM((2, GWH_HALF, HID), F32),
-            dma((6,)), dma((NB,)), dma, dma, dma((21,)), dma((11,)), dma((42,)), dma((11,)),
+            dma((6,)), dma((NB,)), dma, dma, dma((42,)), dma((11,)), dma((42,)), dma((11,)),
             dma((3,)), dma((9,)), dma((3,)), dma((9,)),
         ],
         compiler_params=pltpu.CompilerParams(collective_id=0, has_side_effects=True, vmem_limit_bytes=64000000),

time: 91.3 us -> 92 us (level)
  no operation moved by 1% of the time
where the time goes in v10:
time: 92 us; the launch traced here: 91.9 us
  Pallas kernels  91.3 us (99%)
    pallas_call x1, Pallas kernels, device_step(): pl.pallas_call(step_kernel, name='gcn_step', out_shape=pltpu.VMEM((OUT_RO...  90.6 us

profile of v10, /device:TPU:0, one launch (start us, length us, event | category | flops | bytes accessed | tf_op | source)
XLA Modules:
  0.0 91.9 jit_solution(1953464554295950062)
XLA Ops:
  0.6 90.6 %gcn_step.1.sums_ref = f32[152,128]{1,0:T(8,128)S(1)} custom-call(bf16[1024,16384]{1,0:T(8,128)(2,1)} %adj_hbm.1, bf16[100,1024]{1,0:T(8,128)(2,1)} %bitcast.6, f32[100,128]{1,0:T(8,128)} %wh_hbm.1, f32[47,128]{1,0:T(8,128)} %bitcast.7, s32[1,1024]{1,0:T(1,128)} %bitcast.8, s32[1,1024]{1,0:T(1,128)} %bitcast.9, s32[16,16]{1,0:T(8,128)} %bm_hbm.1), custom_call_target="tpu_custom_call" | custom-call | tf_op jit(solution)/shard_map/gcn_step/pallas_call | solution.py:457
  91.3 0.6 split_sums.1

commit v11 on v8

--- a/solution.py
+++ b/solution.py
@@ -18,8 +18,7 @@
 ORDERS = [(1, 2, 4), (2, 4, 1), (4, 1, 2)]
 X_CHUNKS = [(0, 40, 0, BLK, 0), (40, 32, 0, BLK, 1), (72, 32, 0, BLK, 2)]
 Y_CHUNKS = [(0, 16, 0, BLK, 0), (16, 16, 0, BLK, 1), (32, 16, 0, BLK, 2)]
-D1_CHUNKS = [(0, 40, 0, BLK, 0), (40, 40, 0, BLK, 1), (80, 40, 0, BLK, 2),
-             (120, 8, 0, 384, 0), (120, 8, 384, 384, 1), (120, 8, 768, 256, 2)]
+D1_CHUNKS = [(0, 48, 0, BLK, 0), (48, 40, 0, BLK, 1), (88, 40, 0, BLK, 2)]
 GWO_HALF, GWH_HALF = 24, 56
 OUT_ROWS = F_PAD + CLS_PAD
 M_TILE = 256
@@ -496,7 +495,7 @@
             pltpu.VMEM((GWH_HALF, HID), F32),
             pltpu.VMEM((8, GWH_HALF, HID), F32),
             pltpu.VMEM((2, GWH_HALF, HID), F32),
-            dma((6,)), dma((NB,)), dma, dma, dma((21,)), dma((11,)), dma((42,)), dma((11,)),
+            dma((6,)), dma((NB,)), dma, dma, dma((21,)), dma((11,)), dma((21,)), dma((11,)),
             dma((3,)), dma((9,)), dma((3,)), dma((9,)),
         ],
         compiler_params=pltpu.CompilerParams(collective_id=0, has_side_effects=True, vmem_limit_bytes=64000000),

time: 91.3 us -> 92.2 us (level)
  no operation moved by 1% of the time
where the time goes in v11:
time: 92.2 us; the launch traced here: 92 us
  Pallas kernels  91.4 us (99%)
    pallas_call x1, Pallas kernels, device_step(): pl.pallas_call(step_kernel, name='gcn_step', out_shape=pltpu.VMEM((OUT_RO...  90.8 us

profile of v11, /device:TPU:0, one launch (start us, length us, event | category | flops | bytes accessed | tf_op | source)
XLA Modules:
  0.0 92.0 jit_solution(7622207818646194337)
XLA Ops:
  0.6 90.8 %gcn_step.1.sums_ref = f32[152,128]{1,0:T(8,128)S(1)} custom-call(bf16[1024,16384]{1,0:T(8,128)(2,1)} %adj_hbm.1, bf16[100,1024]{1,0:T(8,128)(2,1)} %bitcast.6, f32[100,128]{1,0:T(8,128)} %wh_hbm.1, f32[47,128]{1,0:T(8,128)} %bitcast.7, s32[1,1024]{1,0:T(1,128)} %bitcast.8, s32[1,1024]{1,0:T(1,128)} %bitcast.9, s32[16,16]{1,0:T(8,128)} %bm_hbm.1), custom_call_target="tpu_custom_call" | custom-call | tf_op jit(solution)/shard_map/gcn_step/pallas_call | solution.py:454
  91.4 0.6 split_sums.1

commit v12 on v8

--- a/solution.py
+++ b/solution.py
@@ -92,7 +92,7 @@
 
 
 def step_kernel(adj_hbm, x_hbm, wh_hbm, wot_hbm, lab_hbm, msk_hbm, bm_hbm, out_ref,
-                x_ref, wh_ref, wot_ref, lab_ref, msk_ref, bm_ref,
+                x_ref, wh_ref, wot_ref, lab_ref, msk_ref, bm_ref, mask_tab,
                 adj, xall, yall, y1b, z1, z1t, z2, z2t, turned, hid, gt, et, con, part2, part1, rb2, rb1, whs, wos, macc, lossv,
                 gwos, gwop, gwor, gwog, gwof, gwhs, gwhp, gwhr, gwhg, gwhf,
                 io_sem, a_sem, ici_send, d2d_send, recv_a, d2d_a, recv_b, d2d_b,
@@ -100,11 +100,16 @@
     me = lax.axis_index(AXIS_NAME)
     coords = [me % 2, (me // 2) % 2, (me // 4) % 2, me // 8]
 
-    def dev(rel):
+    def device_of(rel):
         total = 0
         for bit in range(4):
             total = total + ((coords[bit] + ((rel >> bit) & 1)) % 2) * (1 << bit)
         return total
+
+    devices = [device_of(rel) for rel in range(NB)]
+
+    def dev(rel):
+        return devices[rel]
 
     def rel_of(slot):
         return 2 * QS[slot // 2] + slot % 2
@@ -147,23 +152,11 @@
     wos[0:CLS, :] = wot_ref[...].astype(BF16)
     pl.semaphore_wait(barrier, len(peers))
 
+    for n in range(NB):
+        mask_tab[n] = bm_ref[me, dev(rel_of(n))]
+
     def mask_of(slot):
-        if isinstance(slot, int):
-            return bm_ref[me, dev(rel_of(slot))]
-        i = slot // 2
-        c = slot % 2
-        bits = []
-        for bit in (1, 2, 4):
-            b = 0
-            for pos, q in enumerate(QS):
-                if q & bit:
-                    d = (i - pos) * (i - pos)
-                    b = b + 1 // (1 + d)
-            bits.append(b)
-        total = ((coords[0] + c) % 2)
-        for n, b in enumerate(bits):
-            total = total + ((coords[n + 1] + b) % 2) * (2 << n)
-        return bm_ref[me, total]
+        return mask_tab[slot]
 
 
     def gather_product(buf, chunks, recv, recv_d2d, ops, swapped, first, dots):
@@ -465,6 +458,7 @@
             pltpu.VMEM((1, BLK), jnp.int32),
             pltpu.VMEM((1, BLK), jnp.int32),
             pltpu.SMEM((NB, NB), jnp.int32),
+            pltpu.SMEM((NB,), jnp.int32),
             pltpu.VMEM((NB, BLK, BLK), BF16),
             pltpu.VMEM((NB, F_PAD, BLK), BF16),
             pltpu.VMEM((NB, CLS_PAD, BLK), BF16),

time: 91.3 us -> 91.8 us (level)
  no operation moved by 1% of the time
where the time goes in v12:
time: 91.8 us; the launch traced here: 91.7 us
  Pallas kernels  91 us (99%)
    pallas_call x1, Pallas kernels, device_step(): pl.pallas_call(step_kernel, name='gcn_step', out_shape=pltpu.VMEM((OUT_RO...  90.4 us

profile of v12, /device:TPU:0, one launch (start us, length us, event | category | flops | bytes accessed | tf_op | source)
XLA Modules:
  0.0 91.7 jit_solution(2521830848871135936)
XLA Ops:
  0.6 90.4 %gcn_step.1.sums_ref = f32[152,128]{1,0:T(8,128)S(1)} custom-call(bf16[1024,16384]{1,0:T(8,128)(2,1)} %adj_hbm.1, bf16[100,1024]{1,0:T(8,128)(2,1)} %bitcast.6, f32[100,128]{1,0:T(8,128)} %wh_hbm.1, f32[47,128]{1,0:T(8,128)} %bitcast.7, s32[1,1024]{1,0:T(1,128)} %bitcast.8, s32[1,1024]{1,0:T(1,128)} %bitcast.9, s32[16,16]{1,0:T(8,128)} %bm_hbm.1), custom_call_target="tpu_custom_call" | custom-call | tf_op jit(solution)/shard_map/gcn_step/pallas_call | solution.py:448
  91.0 0.6 split_sums.1
